TPU v7x, 8 devices: a whole 2x2x1 slice. The times are simulated.
8 devices in a mesh: dp: 4 (over z, y, x), tp: 2 (over core).
Axes of the slice: x: 2, y: 2, z: 1, core: 2. Of those that a mesh axis runs over, the one named last changes fastest.
Arguments:
- block_in: bfloat16 [3, 8, 2048, 1408], P(None, 'dp')
- pre_act: bfloat16 [3, 8, 2048, 6144], P(None, 'dp', None, 'tp')
- w_in: bfloat16 [3, 1408, 6144], P(None, None, 'tp')
- w_out: bfloat16 [3, 6144, 1408], P(None, 'tp')
- d_out: bfloat16 [8, 2048, 1408], P('dp')
- noise_in: float32 [3, 1408, 6144], P(None, None, 'tp')
- noise_out: float32 [3, 6144, 1408], P(None, 'tp')
- clip_norm: float32 [], replicated
- noise_mult: float32 [], replicated
Outputs:
- output 1: float32 [3, 1408, 6144], P(None, None, 'tp')
- output 2: float32 [3, 6144, 1408], P(None, 'tp')
All inputs are finite; a program needn't handle non-finite values.
Results may differ from a plain program's by a relative error of at most 0.00950181.
Values are sent between devices in bfloat16 or wider.
A program may use at most 1.5 GiB of HBM per device.

v0:
```python
import functools

import jax
import jax.numpy as jnp
from jax import lax
from jax.experimental import pallas as pl
from jax.experimental.pallas import tpu as pltpu
from jax.sharding import PartitionSpec as P


INV_SQRT2 = 0.7071067811865476
INV_SQRT_2PI = 0.3989422804014327
LOG2_E = 1.4426950408889634
F_BLOCK = 512
T_CHUNK = 256
IN_SLOTS = 4
LOAD_CHUNKS = 2
MIX_ROWS = 32
N_SUM, N_FIRST, N_PUT = 20, 12, 32
VMEM_LIMIT = 67_000_000

F32 = jnp.float32
BF16 = jnp.bfloat16
ANY = pl.ANY
MESH = pl.DeviceIdType.MESH


def dot_nn(a, b):
    return lax.dot_general(a, b, (((1,), (0,)), ((), ())), preferred_element_type=F32)


def dot_nt(a, b):
    return lax.dot_general(a, b, (((1,), (1,)), ((), ())), preferred_element_type=F32)


def block_at(j, n_half, x_pos, y_pos):
    far = n_half * (1 - y_pos) + x_pos * j + (1 - x_pos) * (n_half - 1 - j)
    own = n_half * y_pos + j - n_half
    is_far = 1 - j // n_half
    return is_far * far + (1 - is_far) * own


def stack_kernel(n_layers, n_ex, n_steps, u_hbm, w1_hbm, w2_hbm, x_hbm, dout_hbm,
                 p_hbm, q_hbm, dzo_hbm, g1k_hbm, g1s_hbm, g1r_hbm, g2k_hbm, g2s_hbm, g2r_hbm,
                 g1l_hbm, g2l_hbm, g1e_hbm, g1er_hbm, g2e_hbm, g2er_hbm, ss_hbm, ss_ref,
                 u_buf, w1_buf, w2_buf, x_t, dz, dz_t, dh, h, acc, x_st, z_st, p_st, q_st, g1_st, g1s_st, g2_st, g2s_st,
                 block_sem, in_sem, out_sem, io_sem, tp_send, tp_recv, far_send, far_recv, ss_send, ss_recv):
    task, step = pl.program_id(0), pl.program_id(1)
    n_early = (n_layers - 1) * n_ex
    n_task = n_early + n_ex
    dp = lax.axis_index('dp')
    x_pos, y_pos = lax.rem(dp, 2), dp // 2
    x_far = {'dp': dp + 1 - 2 * x_pos}
    y_far = {'dp': dp + 2 - 4 * y_pos}
    tp_far = {'tp': 1 - lax.axis_index('tp')}
    n_tok, d_model = dz.shape
    half_d, quarter_d = d_model // 2, d_model // 4
    n_half = n_steps // 2
    half_b = F_BLOCK // 2
    n_t = n_tok // T_CHUNK
    example = lax.rem(task, n_ex)
    cols = lambda k: pl.ds(pl.multiple_of(k * F_BLOCK, F_BLOCK), F_BLOCK)
    chunk = lambda c: pl.ds(c * T_CHUNK if isinstance(c, int) else pl.multiple_of(c * T_CHUNK, T_CHUNK), T_CHUNK)

    def fetch(act, t, j, slot):
        layer, at = n_layers - 1 - t // n_ex, cols(block_at(j, n_half, x_pos, y_pos))

        def one(k, src, dst):
            getattr(pltpu.make_async_copy(src, dst.at[slot], block_sem.at[k, slot]), act)()

        one(0, u_hbm.at[layer, lax.rem(t, n_ex), :, at], u_buf)
        one(1, w2_hbm.at[layer, at, :], w2_buf)
        pl.when(t < n_early)(lambda: one(2, w1_hbm.at[layer, :, at], w1_buf))

    ends = (step + 1) // n_steps
    now = lax.rem(task * n_steps + step, 2)

    def rarely(cond, body, n=1):
        def trip(i, carry):
            body(i)
            return carry

        lax.fori_loop(0, jnp.where(cond, n, 0), trip, 0)

    is_first = (task == 0) & (step == 0)
    rarely(is_first, lambda i: fetch('start', task, step, now))
    pl.when(task + ends < n_task)(lambda: fetch('start', task + ends, step + 1 - n_steps * ends, 1 - now))

    def in_start(t, c):
        slot, rows, ex = lax.rem(c, IN_SLOTS), chunk(c), lax.rem(t, n_ex)
        copy = lambda k, src, dst: pltpu.make_async_copy(src, dst.at[slot], in_sem.at[k, slot]).start()
        copy(0, x_hbm.at[n_layers - 1 - t // n_ex, ex, rows, :], x_st)

        @pl.when(t < n_early)
        def _():
            copy(1, dout_hbm.at[ex, rows, :], z_st)

        @pl.when(t >= n_early)
        def _():
            copy(1, dzo_hbm.at[ex, rows, :], z_st)

        @pl.when(t >= n_ex)
        def _():
            copy(2, p_hbm.at[t - n_ex, rows, :], p_st)
            copy(3, q_hbm.at[t - n_ex, rows, :], q_st)

    def in_wait(c):
        slot, rows = lax.rem(c, IN_SLOTS), chunk(c)
        wait = lambda k, dst: pltpu.make_async_copy(dout_hbm.at[0, rows, :], dst.at[slot], in_sem.at[k, slot]).wait()
        wait(0, x_st)
        wait(1, z_st)

        @pl.when(task >= n_ex)
        def _():
            wait(2, p_st)
            wait(3, q_st)

    def tp_copy(t):
        return pltpu.make_async_remote_copy(
            src_ref=p_hbm.at[t], dst_ref=q_hbm.at[t], send_sem=tp_send.at[t], recv_sem=tp_recv.at[t],
            device_id=tp_far, device_id_type=MESH)

    def front(load, to_dx):
        n_in = LOAD_CHUNKS if load and not to_dx else n_t

        def trip(i, carry):
            def dx_part(rows):
                part = dot_nt(dh[rows, :], w1_buf[now])
                acc[rows, :] = part if load else acc[rows, :] + part

            for s in range(n_in):
                c = i * n_in + s
                rows = chunk(c)
                if load:
                    @pl.when(c + IN_SLOTS - 1 < n_t)
                    def _():
                        in_start(task, c + IN_SLOTS - 1)

                    in_wait(c)
                    slot = lax.rem(c, IN_SLOTS)
                    z = z_st[slot]
                    moved = (z.astype(F32) + (p_st[slot].astype(F32) + q_st[slot].astype(F32))).astype(BF16)
                    z = jnp.where(task >= n_ex, moved, z) if to_dx else moved
                    dz[rows, :] = z
                    dz_t[:, rows] = z.T
                    x_t[:, rows] = x_st[slot].T
                u = u_buf[now, rows, :].astype(F32)
                t = u * INV_SQRT2
                cdf = 0.5 * lax.erf(t) + 0.5
                h[rows, :] = (u * cdf).astype(BF16)
                slope = cdf + (t * (INV_SQRT_2PI / INV_SQRT2)) * jnp.exp2((t * t) * -LOG2_E)
                dh[rows, :] = (slope * dot_nt(dz[rows, :], w2_buf[now])).astype(BF16)
                if to_dx and s:
                    dx_part(chunk(c - 1))
            if to_dx:
                dx_part(chunk(i * n_in + n_in - 1))
            return carry

        if n_in == n_t:
            trip(0, 0)
        else:
            lax.fori_loop(0, n_t // n_in, trip, 0)

    def begin(c):
        ss_ref[...] = jnp.zeros_like(ss_ref)
        in_start(task, c)

    rarely(is_first, begin, IN_SLOTS - 1)

    fetch('wait', task, step, now)
    for load in (True, False):
        for to_dx in (True, False):
            @pl.when(((step == 0) if load else (step > 0)) & ((task < n_early) if to_dx else (task >= n_early)))
            def _():
                front(load, to_dx)

    dz_keep = pltpu.make_async_copy(dz, dzo_hbm.at[example], io_sem.at[0])
    is_mid = (task >= n_ex) & (task < n_early)
    pl.when(is_mid & (step == 0))(dz_keep.start)
    ends_early = (step == n_steps - 1) & (task < n_early)
    dx_out = pltpu.make_async_copy(dz, p_hbm.at[task], io_sem.at[1])

    @pl.when(ends_early)
    def _():
        pl.when(is_mid)(dz_keep.wait)

        def put(c, carry):
            dz[chunk(c), :] = acc[chunk(c), :].astype(BF16)
            return carry

        lax.fori_loop(0, n_t, put, 0)
        dx_out.start()

    def far_copy(axis, src, dst):
        return pltpu.make_async_remote_copy(
            src_ref=src, dst_ref=dst, send_sem=far_send.at[axis], recv_sem=far_recv.at[axis],
            device_id=y_far if axis % 2 else x_far, device_id_type=MESH)

    own_rows = pl.ds(pl.multiple_of(x_pos * half_d, 16), half_d)
    pass_rows = pl.ds(pl.multiple_of((1 - y_pos) * quarter_d, 16), quarter_d)
    cut_half = pl.ds(pl.multiple_of((1 - x_pos) * half_b, half_b), half_b)
    to_half = pl.ds(pl.multiple_of(x_pos * F_BLOCK, half_b), half_b)
    to_full = pl.ds(pl.multiple_of((1 - x_pos) * half_b, half_b), F_BLOCK)

    def block(act, t, j):
        far_k = x_pos * j + (1 - x_pos) * (n_half - 1 - j)
        far_at, own_at = cols(far_k), cols(j - n_half)
        fb_at = cols(block_at(j, n_half, x_pos, y_pos))

        def local(n, src, dst):
            cp = pltpu.make_async_copy(src, dst, out_sem.at[n])
            (cp.start if act == 'start' else cp.wait)()

        def far(axis, src, dst):
            if act == 'end':
                far_copy(axis, src, dst).start()

        @pl.when(t < n_early)
        def _():
            local(0, g1_st.at[own_rows, :], g1k_hbm.at[t, :, fb_at])
            local(1, g1s_st, g1s_hbm.at[t, :, fb_at])
            far(0, g1s_hbm.at[t, :, fb_at], g1r_hbm.at[t, :, fb_at])

            @pl.when(j < n_half)
            def _():
                local(2, g2s_st, g2s_hbm.at[t, :, far_at])
                far(1, g2s_hbm.at[t, :, far_at], g2r_hbm.at[t, :, far_at])

            @pl.when(j >= n_half)
            def _():
                local(3, g2_st, g2k_hbm.at[t, :, own_at])

        @pl.when(t >= n_early)
        def _():
            ex = t - n_early
            local(1, g1s_st.at[pass_rows, :], g1e_hbm.at[ex, :, fb_at])
            pl.when((t < n_task - 1) | (j < n_steps - 1))(lambda: far(2, g1e_hbm.at[ex, :, fb_at], g1er_hbm.at[ex, :, fb_at]))
            local(0, g1_st, g1l_hbm.at[ex, :, fb_at])
            local(3, g2_st, g2l_hbm.at[ex, :, fb_at])

            @pl.when(j == 0)
            def _():
                local(2, g2s_st, g2e_hbm.at[ex, :, to_full])
                far(3, g2e_hbm.at[ex, :, to_full], g2er_hbm.at[ex, :, to_full])

            @pl.when(j == 1)
            def _():
                local(2, g2s_st.at[:, cut_half], g2e_hbm.at[ex, :, to_half])
                far(3, g2e_hbm.at[ex, :, to_half], g2er_hbm.at[ex, :, to_half])

    @pl.when((task > 0) | (step > 0))
    def _():
        block('end', jnp.where(step > 0, task, task - 1), jnp.where(step > 0, step - 1, n_steps - 1))

    def square(g):
        return jnp.sum((g * g).reshape(g.shape[0] // 8, 8, g.shape[1]), axis=0)

    total = ss_ref[example]
    for r in range(2):
        part = pl.ds(r * quarter_d, quarter_d)
        own = pl.ds(pl.multiple_of(r * quarter_d + x_pos * half_d, 16), quarter_d)
        far = pl.ds(pl.multiple_of(r * quarter_d + (1 - x_pos) * half_d, 16), quarter_d)
        g = dot_nn(x_t[own, :], dh[...])
        g1_st[own, :] = g
        total = total + square(g)
        g = dot_nn(x_t[far, :], dh[...])
        g1_st[far, :] = g
        g1s_st[part, :] = g.astype(BF16)
        total = total + square(g)
        for at in (part, pl.ds(r * quarter_d + half_d, quarter_d)):
            g = dot_nn(dz_t[at, :], h[...])
            g2_st[at, :] = g
            g2s_st[at, :] = g.astype(BF16)
            total = total + square(g)
    ss_ref[example] = total
    block('start', task, step)
    ends_all = (step == n_steps - 1) & (task == n_task - 1)

    def last_far(i):
        at = cols(block_at(step, n_half, x_pos, y_pos))
        far_copy(2, g1s_st.at[pass_rows, :], g1er_hbm.at[n_ex - 1, :, at]).start()

    rarely(ends_all, last_far)

    @pl.when(ends_early)
    def _():
        dx_out.wait()
        tp_copy(task).start()

    ends_task = (step == n_steps - 1) & (task < n_task - 1)
    rarely(ends_task & (task + 1 >= n_ex), lambda i: tp_copy(task + 1 - n_ex).wait())
    rarely(ends_task, lambda c: in_start(task + 1, c), IN_SLOTS - 1)

    def finish(i):
        keep = pltpu.make_async_copy(ss_ref, ss_hbm.at[0], io_sem.at[0])
        keep.start()
        keep.wait()
        tp = lax.axis_index('tp')
        peers = [
            {'dp': dp, 'tp': 1 - tp}, {**x_far, 'tp': tp}, {**x_far, 'tp': 1 - tp}, {**y_far, 'tp': tp}, {**y_far, 'tp': 1 - tp}]
        sums = [
            pltpu.make_async_remote_copy(
                src_ref=ss_hbm.at[0], dst_ref=ss_hbm.at[k + 1], send_sem=ss_send.at[k], recv_sem=ss_recv.at[k],
                device_id=peer, device_id_type=MESH)
            for k, peer in enumerate(peers)]
        for cp in sums:
            cp.start()
        block('end', task, step)
        for cp in sums:
            cp.wait()
        far_copy(0, g1s_hbm, g1r_hbm).wait()
        far_copy(1, g2s_hbm, g2r_hbm).wait()
        far_copy(2, g1e_hbm, g1er_hbm).wait()
        far_copy(3, g2e_hbm, g2er_hbm).wait()

    rarely(ends_all, finish)


def run_stack(pre_act, w_in, w_out, block_in, d_out):
    n_layers, n_ex, n_tok, d_model = block_in.shape
    d_ff = pre_act.shape[3]
    n_steps = d_ff // F_BLOCK
    half_d, half_f = d_model // 2, d_ff // 2
    n_early = (n_layers - 1) * n_ex
    sds = jax.ShapeDtypeStruct
    outs = [
        sds((n_early, n_tok, d_model), BF16), sds((n_early, n_tok, d_model), BF16), sds((n_ex, n_tok, d_model), BF16),
        sds((n_early, half_d, d_ff), F32), sds((n_early, half_d, d_ff), BF16), sds((n_early, half_d, d_ff), BF16),
        sds((n_early, d_model, half_f), F32), sds((n_early, d_model, half_f), BF16), sds((n_early, d_model, half_f), BF16),
        sds((n_ex, d_model, d_ff), F32), sds((n_ex, d_model, d_ff), F32),
        sds((n_ex, d_model // 4, d_ff), BF16), sds((n_ex, d_model // 4, d_ff), BF16),
        sds((n_ex, d_model, d_ff // 4), BF16), sds((n_ex, d_model, d_ff // 4), BF16),
        sds((6, n_ex, 8, F_BLOCK), F32),
    ]
    out_specs = [pl.BlockSpec(memory_space=ANY)] * len(outs)
    vm = pltpu.VMEM
    scratch = [
        vm((n_ex, 8, F_BLOCK), F32),
        vm((2, n_tok, F_BLOCK), BF16), vm((2, d_model, F_BLOCK), BF16), vm((2, F_BLOCK, d_model), BF16),
        vm((d_model, n_tok), BF16), vm((n_tok, d_model), BF16), vm((d_model, n_tok), BF16),
        vm((n_tok, F_BLOCK), BF16), vm((n_tok, F_BLOCK), BF16), vm((n_tok, d_model), F32),
        *[vm((IN_SLOTS, T_CHUNK, d_model), BF16)] * 4,
        vm((d_model, F_BLOCK), F32), vm((half_d, F_BLOCK), BF16), vm((d_model, F_BLOCK), F32), vm((d_model, F_BLOCK), BF16),
        pltpu.SemaphoreType.DMA((3, 2)),
        pltpu.SemaphoreType.DMA((4, IN_SLOTS)), pltpu.SemaphoreType.DMA((4,)), pltpu.SemaphoreType.DMA((2,)),
        pltpu.SemaphoreType.DMA((n_early,)), pltpu.SemaphoreType.DMA((n_early,)),
        pltpu.SemaphoreType.DMA((4,)), pltpu.SemaphoreType.DMA((4,)),
        pltpu.SemaphoreType.DMA((5,)), pltpu.SemaphoreType.DMA((5,)),
    ]
    n_dots = 4 * n_early + 3 * n_ex
    return pl.pallas_call(
        functools.partial(stack_kernel, n_layers, n_ex, n_steps),
        out_shape=outs,
        grid_spec=pltpu.PrefetchScalarGridSpec(
            num_scalar_prefetch=0, grid=(n_early + n_ex, n_steps), in_specs=[pl.BlockSpec(memory_space=ANY)] * 5, out_specs=out_specs, scratch_shapes=scratch),
        compiler_params=pltpu.CompilerParams(
            dimension_semantics=('arbitrary', 'arbitrary'), vmem_limit_bytes=VMEM_LIMIT, has_side_effects=True),
        cost_estimate=pl.CostEstimate(
            flops=2 * n_dots * n_tok * d_model * d_ff, bytes_accessed=500_000_000, transcendentals=2 * n_tok * d_ff),
        name='stack',
    )(pre_act, w_in, w_out, block_in, d_out)


def norm_kernel(sq_ref, out_ref):
    for d in range(out_ref.shape[0]):
        for ex in range(out_ref.shape[1]):
            out_ref[d, ex] = jnp.sum(sq_ref[2 * d, ex] + sq_ref[2 * d + 1, ex])


def chip_norms(squares):
    return pl.pallas_call(
        norm_kernel,
        out_shape=jax.ShapeDtypeStruct((3, squares.shape[1]), F32),
        in_specs=[pl.BlockSpec(memory_space=pltpu.VMEM)],
        out_specs=pl.BlockSpec(memory_space=pltpu.SMEM),
        name='norms',
    )(squares)


def mix_kernel(factors, sc_ref, clip_ref, *refs):
    def group(r, carry):
        rows = pl.ds(pl.multiple_of(r * MIX_ROWS, MIX_ROWS), MIX_ROWS)
        total = None
        for at, ref in zip(factors, refs):
            value = ref[0, rows, :].astype(F32)
            if at is not None:
                value = value * clip_ref[at[0], at[1]]
            total = value if total is None else total + value
        refs[-1][rows, :] = total.astype(BF16)
        return carry

    lax.fori_loop(0, refs[-1].shape[0] // MIX_ROWS, group, 0)


def mix(which, shape, terms, clip, before, part, n_parts):
    rows, width = shape
    part_width = width // n_parts
    block = (rows, width // 4) if which == 0 else (rows // 4, part_width)
    n_blocks = 4 // n_parts if which == 0 else 4

    def spec(k, v, lead):
        off = part * n_blocks if which == 0 and v.shape[2] > part_width else 0
        if which == 0:
            return pl.BlockSpec((1, *block), lambda i, sc: (lead, sc[k], i + off))
        return pl.BlockSpec((1, *block), lambda i, sc: (lead, i, sc[k]))

    def place(v, p):
        return p * n_parts + part if which == 1 and v.shape[2] > part_width else p

    out_map = (lambda i, sc: (0, i)) if which == 0 else (lambda i, sc: (i, 0))
    places = jnp.stack([jnp.asarray(place(v, p), jnp.int32) for v, _, p, _ in terms])
    if before is not None:
        places, _ = lax.optimization_barrier((places, before))
    return pl.pallas_call(
        functools.partial(mix_kernel, [at for _, _, _, at in terms]),
        out_shape=jax.ShapeDtypeStruct((rows, part_width), BF16),
        grid_spec=pltpu.PrefetchScalarGridSpec(
            num_scalar_prefetch=1, grid=(n_blocks,),
            in_specs=[pl.BlockSpec(memory_space=pltpu.SMEM)] + [spec(k, v, lead) for k, (v, lead, _, _) in enumerate(terms)],
            out_specs=pl.BlockSpec(block, out_map)),
        compiler_params=pltpu.CompilerParams(dimension_semantics=('arbitrary',), vmem_limit_bytes=40_000_000),
        cost_estimate=pl.CostEstimate(
            flops=2 * len(terms) * rows * part_width, bytes_accessed=14 * rows * part_width, transcendentals=0),
        name='mix',
    )(places, clip, *[v for v, _, _, _ in terms])


def put_in_kernel(sc_ref, coef_ref, piece_ref, noise_ref, *rest):
    out_ref = rest[-1]

    def group(r, carry):
        rows = pl.ds(pl.multiple_of(r * 16, 16), 16)
        out_ref[0, 0, rows, :] = (piece_ref[rows, :].astype(F32) + coef_ref[0] * noise_ref[0, 0, rows, :]) * coef_ref[1]
        return carry

    lax.fori_loop(0, piece_ref.shape[0] // 16, group, 0)


def put_out_kernel(sc_ref, coef_ref, piece_ref, noise_ref, *rest):
    out_ref = rest[-1]

    def group(r, carry):
        at = pl.ds(pl.multiple_of(r * 128, 128), 128)
        out_ref[0, 0, :, at] = (piece_ref[at, :].astype(F32).T + coef_ref[0] * noise_ref[0, 0, :, at]) * coef_ref[1]
        return carry

    lax.fori_loop(0, piece_ref.shape[0] // 128, group, 0, unroll=piece_ref.shape[1] == 128)


def put_piece(transposed, total, layer, quarter, part, coef, piece, noise):
    if transposed:
        rows, width = piece.shape[1], piece.shape[0]
        block = 256 if rows % 256 == 0 else 128
        first = part * (rows // block)
        piece_spec = pl.BlockSpec((width, block), lambda i, sc: (0, i))
        big_spec = pl.BlockSpec((1, 1, block, width), lambda i, sc: (sc[0], sc[1], first + i, 0))
    else:
        rows, width = piece.shape
        block = rows // 2
        piece_spec = pl.BlockSpec((block, width), lambda i, sc: (i, 0))
        big_spec = pl.BlockSpec((1, 1, block, width), lambda i, sc: (sc[0], sc[1], i, part))
    args = [jnp.stack([jnp.int32(layer), quarter]), coef, piece, noise]
    in_specs = [pl.BlockSpec(memory_space=pltpu.SMEM), piece_spec, big_spec]
    aliases = {}
    if total is not None:
        args.append(total)
        in_specs.append(pl.BlockSpec(memory_space=ANY))
        aliases = {4: 0}
    return pl.pallas_call(
        put_out_kernel if transposed else put_in_kernel,
        out_shape=jax.ShapeDtypeStruct(noise.shape, F32),
        grid_spec=pltpu.PrefetchScalarGridSpec(
            num_scalar_prefetch=1, grid=(rows // block,), in_specs=in_specs, out_specs=big_spec),
        input_output_aliases=aliases,
        compiler_params=pltpu.CompilerParams(dimension_semantics=('arbitrary',), vmem_limit_bytes=40_000_000),
        cost_estimate=pl.CostEstimate(flops=4 * rows * width, bytes_accessed=10 * rows * width, transcendentals=0),
        name='put_out' if transposed else 'put_in',
    )(*args)


def solution(mesh):
    data_size = mesh.shape['dp']
    swap_x = [(i, i ^ 1) for i in range(data_size)]
    swap_y = [(i, i ^ 2) for i in range(data_size)]

    def local_step(block_in, pre_act, w_in, w_out, d_out, noise_in, noise_out, clip_norm, noise_mult):
        n_layers, local_batch, _, d_model = block_in.shape
        d_ff = pre_act.shape[3]
        batch_total = local_batch * data_size
        dp = lax.axis_index('dp')
        x_pos, y_pos = lax.rem(dp, 2), dp // 2
        over_x = lambda v: lax.ppermute(v, 'dp', swap_x)
        over_y = lambda v: lax.ppermute(v, 'dp', swap_y)
        res = run_stack(pre_act, w_in, w_out, block_in, d_out)
        g1k, _, g1r, g2k, _, g2r, g1l, g2l, _, g1er, _, g2er, squares = res[3:]
        clip = jnp.minimum(1.0, clip_norm / jnp.sqrt(chip_norms(squares)))
        coef = jnp.stack([noise_mult * clip_norm, jnp.float32(1.0 / batch_total)])

        noise_in4 = noise_in.reshape(n_layers, 4, d_model // 4, d_ff)
        noise_out4 = noise_out.reshape(n_layers, 4, d_ff // 4, d_model)

        shapes = ((d_model // 4, d_ff), (d_model, d_ff // 4))
        at_half, at_side = (x_pos, y_pos), (y_pos, x_pos)
        over_half, over_side = (over_x, over_y), (over_y, over_x)
        early, early_far, late = (g1k, g2k), (g1r, g2r), (g1l, g2l)

        def own_terms(layer, which, half_pos, pos):
            if layer == 0:
                return [(late[which], k, 2 * half_pos + pos, (0, k)) for k in range(local_batch)]
            first = (n_layers - 1 - layer) * local_batch
            return [(early[which], first + k, pos, (0, k)) for k in range(local_batch)]

        made = []

        def mixed(which, terms, part, n_parts):
            made.append(mix(which, shapes[which], terms, clip, made[-1] if made else None, part, n_parts))
            return made[-1]

        def pair_terms(layer, which, part, to_send, *more):
            pos = 1 - at_side[which] if to_send else at_side[which]
            terms = own_terms(layer, which, at_half[which], pos)
            if layer == 0 and not to_send:
                more = (far_last[part, which], *more)
            elif layer == 0:
                terms += [((g1er, g2er)[which], k, 0, (1 + which, k)) for k in range(local_batch)]
            else:
                first = (n_layers - 1 - layer) * local_batch
                terms += [(early_far[which], first + k, pos, (1 + which, k)) for k in range(local_batch)]
            return terms + [(v[None], 0, 0, None) for v in more]

        last = [(0, part, 2) for part in range(2)]
        turns = [(layer, 0, 1) for layer in range(n_layers - 1, 0, -1)] + last
        got, far_last, places = {}, {}, {}
        for _, part, n_parts in last:
            for which in (1, 0):
                terms = own_terms(0, which, 1 - at_half[which], at_side[which])
                far_last[part, which] = over_half[which](mixed(which, terms, part, n_parts))
        for layer, part, n_parts in turns:
            for which in (1, 0):
                value = mixed(which, pair_terms(layer, which, part, True), part, n_parts)
                got[layer, part, which] = over_side[which](value)
        n_first = len(made)
        for layer, part, n_parts in turns:
            for which in (1, 0):
                half_pos, pos = at_half[which], at_side[which]
                own = mixed(which, pair_terms(layer, which, part, False, got[layer, part, which]), part, n_parts)
                near = over_side[which](own)
                side = over_half[which](own)
                diag = over_half[which](near)
                places[layer, part, which] = (
                    (2 * half_pos + pos, own), (2 * half_pos + 1 - pos, near),
                    (2 * (1 - half_pos) + pos, side), (2 * (1 - half_pos) + 1 - pos, diag))
        order = [(turn, which, 0) for turn in turns for which in (1, 0)]
        order += [(turn, which, kind) for turn in turns for kind in (1, 2) for which in (1, 0)]
        order += [(turn, which, 3) for turn in turns for which in (1, 0)]
        grads, noises = [None, None], (noise_in4, noise_out4)
        for (layer, part, _), which, kind in order:
            at, piece = places[layer, part, which][kind]
            grads[which] = put_piece(which == 1, grads[which], layer, at, part, coef, piece, noises[which])
        grad_in, grad_out = grads
        assert (len(made), n_first, len(order)) == (N_SUM, N_FIRST, N_PUT)
        return grad_in.reshape(n_layers, d_model, d_ff), grad_out.reshape(n_layers, d_ff, d_model)

    return jax.shard_map(
        local_step,
        mesh=mesh,
        in_specs=(P(None, 'dp', None, None), P(None, 'dp', None, 'tp'), P(None, None, 'tp'), P(None, 'tp', None),
                  P('dp', None, None), P(None, None, 'tp'), P(None, 'tp', None), P(), P()),
        out_specs=(P(None, None, 'tp'), P(None, 'tp', None)),
        check_vma=False,
    )
```

profile of v0, /device:TPU:0, one launch (start us, length us, event | category | flops | bytes accessed | tf_op | source)
XLA Modules:
  0.0 1321.6 jit_solution(5153345408664597759)
XLA Ops:
  0.7 509.7 %stack.311 = (bf16[4,2048,1408]{2,1,0:T(8,128)(2,1)}, bf16[4,2048,1408]{2,1,0:T(8,128)(2,1)}, bf16[2,2048,1408]{2,1,0:T(8,128)(2,1)}, f32[4,704,3072]{2,1,0:T(8,...) custom-call(bf16[3,2,2048,3072]{3,2,1,0:T(8,128)(2,1)} %u_hbm.1, ...), custom_call_target="tpu_custom_call" | custom-call | flops 389768282112 | bytes 500000000 | tf_op jit(solution)/shard_map/stack/pallas_call | solution.py:351
  513.5 4.8 mix.20
  522.2 4.8 mix.22
  531.1 7.4 mix.24
  539.0 7.5 mix.25
  548.0 7.5 mix.26
  556.9 7.5 mix.27
  572.1 85.3 %collective-permute-done.5 = bf16[1408,384]{1,0:T(8,128)(2,1)S(1)} collective-permute-done((bf16[1408,384]{1,0:T(8,128)(2,1)S(1)}, bf16[1408,384]{1,0:T(8,128)(2,1)S(1)}, u32[]{:S(2)}, u32[]{:S(2)}) %collective-permute-start.5) | collective-permute-done | bytes 1081376 | tf_op jit(solution)/shard_map/ppermute | solution.py:492
  666.3 5.0 mix.30
  680.8 6.5 mix.32.piece_ref
  687.4 7.3 mix.33.piece_ref
  694.7 7.1 mix.34.piece_ref
  701.8 8.7 mix.35.piece_ref
  722.7 8.1 collective-permute-done.8
  735.7 18.1 %collective-permute-done.11 = bf16[352,1536]{1,0:T(8,128)(2,1)S(1)} collective-permute-done((bf16[352,1536]{1,0:T(8,128)(2,1)}, bf16[352,1536]{1,0:T(8,128)(2,1)S(1)}, u32[]{:S(2)}, u32[]{:S(2)}) %collective-permute-start.11) | collective-permute-done | bytes 1081376 | tf_op jit(solution)/shard_map/ppermute | solution.py:493
  755.8 9.4 collective-permute-done.26.piece_ref
  765.6 11.3 collective-permute-done.33.piece_ref
  778.4 10.0 collective-permute-done.24.piece_ref
  793.2 6.9 collective-permute-done.32.piece_ref
  802.6 20.9 %collective-permute-done.14.piece_ref = bf16[352,1536]{1,0:T(8,128)(2,1)} collective-permute-done((bf16[352,1536]{1,0:T(8,128)(2,1)S(1)}, bf16[352,1536]{1,0:T(8,128)(2,1)}, u32[]{:S(2)}, u32[]{:S(2)}) %collective-permute-start.14) | collective-permute-done | bytes 1081376 | tf_op jit(solution)/shard_map/ppermute | solution.py:493
  827.4 63.9 %collective-permute-done.12.piece_ref = bf16[352,1536]{1,0:T(8,128)(2,1)} collective-permute-done((bf16[352,1536]{1,0:T(8,128)(2,1)S(1)}, bf16[352,1536]{1,0:T(8,128)(2,1)}, u32[]{:S(2)}, u32[]{:S(2)}) %collective-permute-start.12) | collective-permute-done | bytes 1081376 | tf_op jit(solution)/shard_map/ppermute | solution.py:493
  892.7 31.3 %collective-permute-done.20.piece_ref = bf16[352,1536]{1,0:T(8,128)(2,1)S(1)} collective-permute-done((bf16[352,1536]{1,0:T(8,128)(2,1)S(1)}, bf16[352,1536]{1,0:T(8,128)(2,1)S(1)}, u32[]{:S(2)}, u32[]{:S(2)}) %collective-permute-start.20) | collective-permute-done | bytes 1081376 | tf_op jit(solution)/shard_map/ppermute | solution.py:492
  930.4 10.8 collective-permute-done.34.piece_ref
  943.0 111.6 %collective-permute-done.27.piece_ref = bf16[1408,384]{1,0:T(8,128)(2,1)S(1)} collective-permute-done((bf16[1408,384]{1,0:T(8,128)(2,1)S(1)}, bf16[1408,384]{1,0:T(8,128)(2,1)S(1)}, u32[]{:S(2)}, u32[]{:S(2)}) %collective-permute-start.27) | collective-permute-done | bytes 1081376 | tf_op jit(solution)/shard_map/ppermute | solution.py:493
  1062.9 42.9 %collective-permute-done.31.piece_ref = bf16[1408,768]{1,0:T(8,128)(2,1)} collective-permute-done((bf16[1408,768]{1,0:T(8,128)(2,1)}, bf16[1408,768]{1,0:T(8,128)(2,1)}, u32[]{:S(2)}, u32[]{:S(2)}) %collective-permute-start.31) | collective-permute-done | bytes 2162720 | tf_op jit(solution)/shard_map/ppermute | solution.py:493
  1106.2 46.0 %collective-permute-done.29.piece_ref = bf16[1408,768]{1,0:T(8,128)(2,1)} collective-permute-done((bf16[1408,768]{1,0:T(8,128)(2,1)}, bf16[1408,768]{1,0:T(8,128)(2,1)}, u32[]{:S(2)}, u32[]{:S(2)}) %collective-permute-start.29) | collective-permute-done | bytes 2162720 | tf_op jit(solution)/shard_map/ppermute | solution.py:493
  1154.9 7.3 put_out.16.rest_0_
  1162.2 7.3 put_out.17.rest_0_
  1174.2 4.6 put_out.19.rest_0_
  1183.4 5.2 put_in.17.rest_0_
  1195.3 7.8 put_out.20.rest_0_
  1203.1 7.3 put_out.21.rest_0_
  1210.4 7.8 put_out.22.rest_0_
  1218.2 7.3 put_out.23.rest_0_
  1225.5 4.6 put_out.24.rest_0_
  1230.1 4.6 put_out.25.rest_0_
  1234.7 4.8 put_out.26.rest_0_
  1239.5 5.2 put_in.20.rest_0_
  1244.7 5.2 put_in.21.rest_0_
  1249.9 5.2 put_in.22.rest_0_
  1255.1 5.2 put_in.23.rest_0_
  1271.0 4.6 put_out.27.rest_0_
  1279.0 7.7 put_out.28.rest_0_
  1286.7 7.7 put_out.29.rest_0_
  1294.4 4.6 put_out.30.rest_0_
  1299.0 4.8 put_out.31
  1303.8 5.2 put_in.28.rest_0_
  1309.0 5.2 put_in.29.rest_0_
  (186 shorter events, 129.8 us)
Async XLA Ops:
  538.5 124.4 %collective-permute-start = (bf16[1408,768]{1,0:T(8,128)(2,1)}, bf16[1408,768]{1,0:T(8,128)(2,1)S(1)}, u32[]{:S(2)}, u32[]{:S(2)}) collective-permute-start(bf16[1408,768]{1,0:T(8,128)(2,1)} %mix.24), channel_id=1, source_target_pairs={{0,2},{2,0},{4,6},{6,4},{1,3},{3,1},{5,7},{7,5}} | collective-permute-start | bytes 6488072 | tf_op jit(solution)/shard_map/ppermute | solution.py:492
  546.5 117.0 %collective-permute-start.1 = (bf16[352,3072]{1,0:T(8,128)(2,1)}, bf16[352,3072]{1,0:T(8,128)(2,1)}, u32[]{:S(2)}, u32[]{:S(2)}) collective-permute-start(bf16[352,3072]{1,0:T(8,128)(2,1)} %mix.25), channel_id=1, source_target_pairs={{0,4},{2,6},{4,0},{6,2},{1,5},{3,7},{5,1},{7,3}} | collective-permute-start | bytes 6488072 | tf_op jit(solution)/shard_map/ppermute | solution.py:493
  555.5 115.8 %collective-permute-start.2 = (bf16[1408,768]{1,0:T(8,128)(2,1)}, bf16[1408,768]{1,0:T(8,128)(2,1)}, u32[]{:S(2)}, u32[]{:S(2)}) collective-permute-start(bf16[1408,768]{1,0:T(8,128)(2,1)} %mix.26), channel_id=1, source_target_pairs={{0,2},{2,0},{4,6},{6,4},{1,3},{3,1},{5,7},{7,5}} | collective-permute-start | bytes 6488072 | tf_op jit(solution)/shard_map/ppermute | solution.py:492
  564.4 108.5 %collective-permute-start.3 = (bf16[352,3072]{1,0:T(8,128)(2,1)}, bf16[352,3072]{1,0:T(8,128)(2,1)}, u32[]{:S(2)}, u32[]{:S(2)}) collective-permute-start(bf16[352,3072]{1,0:T(8,128)(2,1)} %mix.27), channel_id=1, source_target_pairs={{0,4},{2,6},{4,0},{6,2},{1,5},{3,7},{5,1},{7,3}} | collective-permute-start | bytes 6488072 | tf_op jit(solution)/shard_map/ppermute | solution.py:493
  565.1 93.7 %slice-start = ((s8[4325376]{0:T(1024)(128)(4,1)}), s8[4194304]{0:T(1024)(128)(4,1)S(1)}, s32[]{:S(2)}) async-start(s8[4325376]{0:T(1024)(128)(4,1)} %bitcast.34), calls=%async_computation | async-start | bytes 8388608
  567.5 91.3 %slice-start.1 = ((s8[4325376]{0:T(1024)(128)(4,1)}), s8[131072]{0:T(1024)(128)(4,1)S(1)}, s32[]{:S(2)}) async-start(s8[4325376]{0:T(1024)(128)(4,1)} %bitcast.34), calls=%async_computation.1 | async-start | bytes 262144
  571.5 85.8 %collective-permute-start.5 = (bf16[1408,384]{1,0:T(8,128)(2,1)S(1)}, bf16[1408,384]{1,0:T(8,128)(2,1)S(1)}, u32[]{:S(2)}, u32[]{:S(2)}) collective-permute-start(bf16[1408,384]{1,0:T(8,128)(2,1)S(1)} %mix.28), channel_id=1, source_target_pairs={{0,2},{2,0},{4,6},{6,4},{1,3},{3,1},{5,7},{7,5}} | collective-permute-start | bytes 3244040 | tf_op jit(solution)/shard_map/ppermute | solution.py:492
  657.3 53.2 %collective-permute-start.4 = (bf16[1408,384]{1,0:T(8,128)(2,1)}, bf16[1408,384]{1,0:T(8,128)(2,1)}, u32[]{:S(2)}, u32[]{:S(2)}) collective-permute-start(bf16[1408,384]{1,0:T(8,128)(2,1)} %mix.20), channel_id=1, source_target_pairs={{0,4},{2,6},{4,0},{6,2},{1,5},{3,7},{5,1},{7,3}} | collective-permute-start | bytes 3244040 | tf_op jit(solution)/shard_map/ppermute | solution.py:493
  662.9 52.4 %collective-permute-start.7 = (bf16[352,1536]{1,0:T(8,128)(2,1)}, bf16[352,1536]{1,0:T(8,128)(2,1)}, u32[]{:S(2)}, u32[]{:S(2)}) collective-permute-start(bf16[352,1536]{1,0:T(8,128)(2,1)} %mix.29), channel_id=1, source_target_pairs={{0,4},{2,6},{4,0},{6,2},{1,5},{3,7},{5,1},{7,3}} | collective-permute-start | bytes 3244040 | tf_op jit(solution)/shard_map/ppermute | solution.py:493
  663.5 52.2 %collective-permute-start.6 = (bf16[352,1536]{1,0:T(8,128)(2,1)}, bf16[352,1536]{1,0:T(8,128)(2,1)}, u32[]{:S(2)}, u32[]{:S(2)}) collective-permute-start(bf16[352,1536]{1,0:T(8,128)(2,1)} %mix.21), channel_id=1, source_target_pairs={{0,2},{2,0},{4,6},{6,4},{1,3},{3,1},{5,7},{7,5}} | collective-permute-start | bytes 3244040 | tf_op jit(solution)/shard_map/ppermute | solution.py:492
  671.3 49.9 %collective-permute-start.9 = (bf16[1408,384]{1,0:T(8,128)(2,1)}, bf16[1408,384]{1,0:T(8,128)(2,1)}, u32[]{:S(2)}, u32[]{:S(2)}) collective-permute-start(bf16[1408,384]{1,0:T(8,128)(2,1)} %mix.30), channel_id=1, source_target_pairs={{0,2},{2,0},{4,6},{6,4},{1,3},{3,1},{5,7},{7,5}} | collective-permute-start | bytes 3244040 | tf_op jit(solution)/shard_map/ppermute | solution.py:492
  672.9 57.9 %collective-permute-start.8 = (bf16[1408,384]{1,0:T(8,128)(2,1)}, bf16[1408,384]{1,0:T(8,128)(2,1)}, u32[]{:S(2)}, u32[]{:S(2)}) collective-permute-start(bf16[1408,384]{1,0:T(8,128)(2,1)} %mix.22), channel_id=1, source_target_pairs={{0,4},{2,6},{4,0},{6,2},{1,5},{3,7},{5,1},{7,3}} | collective-permute-start | bytes 3244040 | tf_op jit(solution)/shard_map/ppermute | solution.py:493
  687.4 101.1 %copy-start.3 = (bf16[1408,768]{1,0:T(8,128)(2,1)}, bf16[1408,768]{1,0:T(8,128)(2,1)S(1)}, u32[]{:S(2)}) copy-start(bf16[1408,768]{1,0:T(8,128)(2,1)S(1)} %mix.32.piece_ref) | copy-start | bytes 6488068
  701.8 189.5 %copy-start.5 = (bf16[1408,768]{1,0:T(8,128)(2,1)}, bf16[1408,768]{1,0:T(8,128)(2,1)S(1)}, u32[]{:S(2)}) copy-start(bf16[1408,768]{1,0:T(8,128)(2,1)S(1)} %mix.34.piece_ref) | copy-start | bytes 6488068
  701.8 9.3 copy-start.30
  710.5 43.3 %collective-permute-start.11 = (bf16[352,1536]{1,0:T(8,128)(2,1)}, bf16[352,1536]{1,0:T(8,128)(2,1)S(1)}, u32[]{:S(2)}, u32[]{:S(2)}) collective-permute-start(bf16[352,1536]{1,0:T(8,128)(2,1)} %mix.31), channel_id=1, source_target_pairs={{0,4},{2,6},{4,0},{6,2},{1,5},{3,7},{5,1},{7,3}} | collective-permute-start | bytes 3244040 | tf_op jit(solution)/shard_map/ppermute | solution.py:493
  715.3 40.0 %collective-permute-start.10 = (bf16[352,1536]{1,0:T(8,128)(2,1)S(1)}, bf16[352,1536]{1,0:T(8,128)(2,1)S(1)}, u32[]{:S(2)}, u32[]{:S(2)}) collective-permute-start(bf16[352,1536]{1,0:T(8,128)(2,1)S(1)} %copy-done.32), channel_id=1, source_target_pairs={{0,2},{2,0},{4,6},{6,4},{1,3},{3,1},{5,7},{7,5}} | collective-permute-start | bytes 3244040 | tf_op jit(solution)/shard_map/ppermute | solution.py:492
  715.7 49.5 %collective-permute-start.26 = (bf16[1408,384]{1,0:T(8,128)(2,1)S(1)}, bf16[1408,384]{1,0:T(8,128)(2,1)S(1)}, u32[]{:S(2)}, u32[]{:S(2)}) collective-permute-start(bf16[1408,384]{1,0:T(8,128)(2,1)S(1)} %mix.36.piece_ref), channel_id=1, source_target_pairs={{0,2},{2,0},{4,6},{6,4},{1,3},{3,1},{5,7},{7,5}} | collective-permute-start | bytes 3244040 | tf_op jit(solution)/shard_map/ppermute | solution.py:492
  721.2 44.0 %copy-start.7 = (bf16[352,1536]{1,0:T(8,128)(2,1)}, bf16[352,1536]{1,0:T(8,128)(2,1)S(1)}, u32[]{:S(2)}) copy-start(bf16[352,1536]{1,0:T(8,128)(2,1)S(1)} %mix.37.piece_ref) | copy-start | bytes 3244036
  721.2 55.8 %collective-permute-start.33 = (bf16[1408,384]{1,0:T(8,128)(2,1)S(1)}, bf16[1408,384]{1,0:T(8,128)(2,1)S(1)}, u32[]{:S(2)}, u32[]{:S(2)}) collective-permute-start(bf16[1408,384]{1,0:T(8,128)(2,1)S(1)} %mix.36.piece_ref), channel_id=1, source_target_pairs={{0,4},{2,6},{4,0},{6,2},{1,5},{3,7},{5,1},{7,3}} | collective-permute-start | bytes 3244040 | tf_op jit(solution)/shard_map/ppermute | solution.py:493
  735.2 58.0 %copy-start.9 = (bf16[1408,384]{1,0:T(8,128)(2,1)}, bf16[1408,384]{1,0:T(8,128)(2,1)S(1)}, u32[]{:S(2)}) copy-start(bf16[1408,384]{1,0:T(8,128)(2,1)S(1)} %mix.38.piece_ref) | copy-start | bytes 3244036
  735.2 53.3 %collective-permute-start.24 = (bf16[1408,384]{1,0:T(8,128)(2,1)S(1)}, bf16[1408,384]{1,0:T(8,128)(2,1)}, u32[]{:S(2)}, u32[]{:S(2)}) collective-permute-start(bf16[1408,384]{1,0:T(8,128)(2,1)S(1)} %mix.38.piece_ref), channel_id=1, source_target_pairs={{0,2},{2,0},{4,6},{6,4},{1,3},{3,1},{5,7},{7,5}} | collective-permute-start | bytes 3244040 | tf_op jit(solution)/shard_map/ppermute | solution.py:492
  753.8 46.3 %collective-permute-start.32 = (bf16[1408,384]{1,0:T(8,128)(2,1)S(1)}, bf16[1408,384]{1,0:T(8,128)(2,1)S(1)}, u32[]{:S(2)}, u32[]{:S(2)}) collective-permute-start(bf16[1408,384]{1,0:T(8,128)(2,1)S(1)} %mix.38.piece_ref), channel_id=1, source_target_pairs={{0,4},{2,6},{4,0},{6,2},{1,5},{3,7},{5,1},{7,3}} | collective-permute-start | bytes 3244040 | tf_op jit(solution)/shard_map/ppermute | solution.py:493
  755.3 68.2 %collective-permute-start.14 = (bf16[352,1536]{1,0:T(8,128)(2,1)S(1)}, bf16[352,1536]{1,0:T(8,128)(2,1)}, u32[]{:S(2)}, u32[]{:S(2)}) collective-permute-start(bf16[352,1536]{1,0:T(8,128)(2,1)S(1)} %mix.37.piece_ref), channel_id=1, source_target_pairs={{0,4},{2,6},{4,0},{6,2},{1,5},{3,7},{5,1},{7,3}} | collective-permute-start | bytes 3244040 | tf_op jit(solution)/shard_map/ppermute | solution.py:493
  765.2 163.6 %copy-start.17 = (bf16[1408,384]{1,0:T(8,128)(2,1)}, bf16[1408,384]{1,0:T(8,128)(2,1)S(1)}, u32[]{:S(2)}) copy-start(bf16[1408,384]{1,0:T(8,128)(2,1)S(1)} %collective-permute-done.26.piece_ref) | copy-start | bytes 3244036
  765.2 58.7 %collective-permute-start.21 = (bf16[352,1536]{1,0:T(8,128)(2,1)S(1)}, bf16[352,1536]{1,0:T(8,128)(2,1)S(1)}, u32[]{:S(2)}, u32[]{:S(2)}) collective-permute-start(bf16[352,1536]{1,0:T(8,128)(2,1)S(1)} %mix.37.piece_ref), channel_id=1, source_target_pairs={{0,2},{2,0},{4,6},{6,4},{1,3},{3,1},{5,7},{7,5}} | collective-permute-start | bytes 3244040 | tf_op jit(solution)/shard_map/ppermute | solution.py:492
  778.0 148.5 %collective-permute-start.30 = (bf16[1408,768]{1,0:T(8,128)(2,1)S(1)}, bf16[1408,768]{1,0:T(8,128)(2,1)}, u32[]{:S(2)}, u32[]{:S(2)}) collective-permute-start(bf16[1408,768]{1,0:T(8,128)(2,1)S(1)} %mix.32.piece_ref), channel_id=1, source_target_pairs={{0,2},{2,0},{4,6},{6,4},{1,3},{3,1},{5,7},{7,5}} | collective-permute-start | bytes 6488072 | tf_op jit(solution)/shard_map/ppermute | solution.py:492
  788.5 138.6 %collective-permute-start.35 = (bf16[1408,768]{1,0:T(8,128)(2,1)S(1)}, bf16[1408,768]{1,0:T(8,128)(2,1)S(1)}, u32[]{:S(2)}, u32[]{:S(2)}) collective-permute-start(bf16[1408,768]{1,0:T(8,128)(2,1)S(1)} %mix.32.piece_ref), channel_id=1, source_target_pairs={{0,4},{2,6},{4,0},{6,2},{1,5},{3,7},{5,1},{7,3}} | collective-permute-start | bytes 6488072 | tf_op jit(solution)/shard_map/ppermute | solution.py:493
  801.1 90.2 %collective-permute-start.12 = (bf16[352,1536]{1,0:T(8,128)(2,1)S(1)}, bf16[352,1536]{1,0:T(8,128)(2,1)}, u32[]{:S(2)}, u32[]{:S(2)}) collective-permute-start(bf16[352,1536]{1,0:T(8,128)(2,1)S(1)} %mix.39.piece_ref), channel_id=1, source_target_pairs={{0,4},{2,6},{4,0},{6,2},{1,5},{3,7},{5,1},{7,3}} | collective-permute-start | bytes 3244040 | tf_op jit(solution)/shard_map/ppermute | solution.py:493
  823.4 105.4 %collective-permute-start.28 = (bf16[1408,768]{1,0:T(8,128)(2,1)S(1)}, bf16[1408,768]{1,0:T(8,128)(2,1)}, u32[]{:S(2)}, u32[]{:S(2)}) collective-permute-start(bf16[1408,768]{1,0:T(8,128)(2,1)S(1)} %mix.34.piece_ref), channel_id=1, source_target_pairs={{0,2},{2,0},{4,6},{6,4},{1,3},{3,1},{5,7},{7,5}} | collective-permute-start | bytes 6488072 | tf_op jit(solution)/shard_map/ppermute | solution.py:492
  824.9 99.2 %collective-permute-start.20 = (bf16[352,1536]{1,0:T(8,128)(2,1)S(1)}, bf16[352,1536]{1,0:T(8,128)(2,1)S(1)}, u32[]{:S(2)}, u32[]{:S(2)}) collective-permute-start(bf16[352,1536]{1,0:T(8,128)(2,1)S(1)} %mix.39.piece_ref), channel_id=1, source_target_pairs={{0,2},{2,0},{4,6},{6,4},{1,3},{3,1},{5,7},{7,5}} | collective-permute-start | bytes 3244040 | tf_op jit(solution)/shard_map/ppermute | solution.py:492
  891.3 49.9 %collective-permute-start.34 = (bf16[1408,768]{1,0:T(8,128)(2,1)S(1)}, bf16[1408,768]{1,0:T(8,128)(2,1)S(1)}, u32[]{:S(2)}, u32[]{:S(2)}) collective-permute-start(bf16[1408,768]{1,0:T(8,128)(2,1)S(1)} %mix.34.piece_ref), channel_id=1, source_target_pairs={{0,4},{2,6},{4,0},{6,2},{1,5},{3,7},{5,1},{7,3}} | collective-permute-start | bytes 6488072 | tf_op jit(solution)/shard_map/ppermute | solution.py:493
  925.1 132.0 %collective-permute-start.18 = (bf16[352,3072]{1,0:T(8,128)(2,1)S(1)}, bf16[352,3072]{1,0:T(8,128)(2,1)}, u32[]{:S(2)}, u32[]{:S(2)}) collective-permute-start(bf16[352,3072]{1,0:T(8,128)(2,1)S(1)} %mix.33.piece_ref), channel_id=1, source_target_pairs={{0,4},{2,6},{4,0},{6,2},{1,5},{3,7},{5,1},{7,3}} | collective-permute-start | bytes 6488072 | tf_op jit(solution)/shard_map/ppermute | solution.py:493
  926.5 131.5 %collective-permute-start.23 = (bf16[352,3072]{1,0:T(8,128)(2,1)S(1)}, bf16[352,3072]{1,0:T(8,128)(2,1)}, u32[]{:S(2)}, u32[]{:S(2)}) collective-permute-start(bf16[352,3072]{1,0:T(8,128)(2,1)S(1)} %mix.33.piece_ref), channel_id=1, source_target_pairs={{0,2},{2,0},{4,6},{6,4},{1,3},{3,1},{5,7},{7,5}} | collective-permute-start | bytes 6488072 | tf_op jit(solution)/shard_map/ppermute | solution.py:492
  928.4 130.0 %collective-permute-start.16 = (bf16[352,3072]{1,0:T(8,128)(2,1)}, bf16[352,3072]{1,0:T(8,128)(2,1)}, u32[]{:S(2)}, u32[]{:S(2)}) collective-permute-start(bf16[352,3072]{1,0:T(8,128)(2,1)} %mix.35.piece_ref), channel_id=1, source_target_pairs={{0,4},{2,6},{4,0},{6,2},{1,5},{3,7},{5,1},{7,3}} | collective-permute-start | bytes 6488072 | tf_op jit(solution)/shard_map/ppermute | solution.py:493
  928.8 125.7 %collective-permute-start.27 = (bf16[1408,384]{1,0:T(8,128)(2,1)S(1)}, bf16[1408,384]{1,0:T(8,128)(2,1)S(1)}, u32[]{:S(2)}, u32[]{:S(2)}) collective-permute-start(bf16[1408,384]{1,0:T(8,128)(2,1)S(1)} %collective-permute-done.26.piece_ref), channel_id=1, source_target_pairs={{0,4},{2,6},{4,0},{6,2},{1,5},{3,7},{5,1},{7,3}} | collective-permute-start | bytes 3244040 | tf_op jit(solution)/shard_map/ppermute | solution.py:493
  942.6 118.9 %collective-permute-start.22 = (bf16[352,3072]{1,0:T(8,128)(2,1)}, bf16[352,3072]{1,0:T(8,128)(2,1)}, u32[]{:S(2)}, u32[]{:S(2)}) collective-permute-start(bf16[352,3072]{1,0:T(8,128)(2,1)} %mix.35.piece_ref), channel_id=1, source_target_pairs={{0,2},{2,0},{4,6},{6,4},{1,3},{3,1},{5,7},{7,5}} | collective-permute-start | bytes 6488072 | tf_op jit(solution)/shard_map/ppermute | solution.py:492
  1055.6 50.2 %collective-permute-start.31 = (bf16[1408,768]{1,0:T(8,128)(2,1)}, bf16[1408,768]{1,0:T(8,128)(2,1)}, u32[]{:S(2)}, u32[]{:S(2)}) collective-permute-start(bf16[1408,768]{1,0:T(8,128)(2,1)} %collective-permute-done.30.piece_ref), channel_id=1, source_target_pairs={{0,4},{2,6},{4,0},{6,2},{1,5},{3,7},{5,1},{7,3}} | collective-permute-start | bytes 6488072 | tf_op jit(solution)/shard_map/ppermute | solution.py:493
  1057.1 95.1 %collective-permute-start.29 = (bf16[1408,768]{1,0:T(8,128)(2,1)}, bf16[1408,768]{1,0:T(8,128)(2,1)}, u32[]{:S(2)}, u32[]{:S(2)}) collective-permute-start(bf16[1408,768]{1,0:T(8,128)(2,1)} %collective-permute-done.28.piece_ref), channel_id=1, source_target_pairs={{0,4},{2,6},{4,0},{6,2},{1,5},{3,7},{5,1},{7,3}} | collective-permute-start | bytes 6488072 | tf_op jit(solution)/shard_map/ppermute | solution.py:493
  1058.0 245.8 %collective-permute-start.19 = (bf16[352,3072]{1,0:T(8,128)(2,1)}, bf16[352,3072]{1,0:T(8,128)(2,1)}, u32[]{:S(2)}, u32[]{:S(2)}) collective-permute-start(bf16[352,3072]{1,0:T(8,128)(2,1)} %collective-permute-done.18.piece_ref), channel_id=1, source_target_pairs={{0,2},{2,0},{4,6},{6,4},{1,3},{3,1},{5,7},{7,5}} | collective-permute-start | bytes 6488072 | tf_op jit(solution)/shard_map/ppermute | solution.py:492
  1058.4 250.7 %collective-permute-start.17 = (bf16[352,3072]{1,0:T(8,128)(2,1)}, bf16[352,3072]{1,0:T(8,128)(2,1)}, u32[]{:S(2)}, u32[]{:S(2)}) collective-permute-start(bf16[352,3072]{1,0:T(8,128)(2,1)} %collective-permute-done.16.piece_ref), channel_id=1, source_target_pairs={{0,2},{2,0},{4,6},{6,4},{1,3},{3,1},{5,7},{7,5}} | collective-permute-start | bytes 6488072 | tf_op jit(solution)/shard_map/ppermute | solution.py:492
  1061.5 237.6 %collective-permute-start.25 = (bf16[1408,384]{1,0:T(8,128)(2,1)}, bf16[1408,384]{1,0:T(8,128)(2,1)}, u32[]{:S(2)}, u32[]{:S(2)}) collective-permute-start(bf16[1408,384]{1,0:T(8,128)(2,1)} %collective-permute-done.24.piece_ref), channel_id=1, source_target_pairs={{0,4},{2,6},{4,0},{6,2},{1,5},{3,7},{5,1},{7,3}} | collective-permute-start | bytes 3244040 | tf_op jit(solution)/shard_map/ppermute | solution.py:493
  1105.8 208.4 %collective-permute-start.15 = (bf16[352,1536]{1,0:T(8,128)(2,1)}, bf16[352,1536]{1,0:T(8,128)(2,1)}, u32[]{:S(2)}, u32[]{:S(2)}) collective-permute-start(bf16[352,1536]{1,0:T(8,128)(2,1)} %collective-permute-done.14.piece_ref), channel_id=1, source_target_pairs={{0,2},{2,0},{4,6},{6,4},{1,3},{3,1},{5,7},{7,5}} | collective-permute-start | bytes 3244040 | tf_op jit(solution)/shard_map/ppermute | solution.py:492
  1152.2 165.7 %collective-permute-start.13 = (bf16[352,1536]{1,0:T(8,128)(2,1)}, bf16[352,1536]{1,0:T(8,128)(2,1)}, u32[]{:S(2)}, u32[]{:S(2)}) collective-permute-start(bf16[352,1536]{1,0:T(8,128)(2,1)} %collective-permute-done.12.piece_ref), channel_id=1, source_target_pairs={{0,2},{2,0},{4,6},{6,4},{1,3},{3,1},{5,7},{7,5}} | collective-permute-start | bytes 3244040 | tf_op jit(solution)/shard_map/ppermute | solution.py:492
  1154.9 7.3 copy-start.6
  1195.3 7.8 copy-start.14
  1210.4 7.8 copy-start.16
  1286.7 7.7 copy-start.28
  (23 other events, 64.9 us)
where the time goes:
time: 1320 us
  Pallas kernels  787 us (60%)
  waiting for transfers between devices  476 us (36%)
  starting transfers between devices  34.6 us (3%)
  local copies, waits for them, and re-layouts  18.4 us (1%)
    pallas_call x1, Pallas kernels, run_stack(): pl.pallas_call(functools.partial(stack_kernel, n_layers, n_ex, n_steps),...  510 us
    ppermute x18, waiting for transfers between devices, local_step(): over_y = lambda v: lax.ppermute(v, 'dp', swap_y)  340 us
    pallas_call x32, Pallas kernels, put_piece(): pl.pallas_call(put_out_kernel if transposed else put_in_kernel, out_shape...  167 us
    ppermute x18, waiting for transfers between devices, local_step(): over_x = lambda v: lax.ppermute(v, 'dp', swap_x)  136 us
    pallas_call x20, Pallas kernels, mix(): pl.pallas_call(functools.partial(mix_kernel, [at for _, _, _, at in terms...  109 us
  transfers between devices with their start and end apart: 36, of which 14 were waited for; matrix products, arithmetic and copies ran while one was open for 0% of the time, Pallas kernels for 19%

commit v1 on v0

--- a/solution.py
+++ b/solution.py
@@ -84,7 +84,6 @@
 
     is_first = (task == 0) & (step == 0)
     rarely(is_first, lambda i: fetch('start', task, step, now))
-    pl.when(task + ends < n_task)(lambda: fetch('start', task + ends, step + 1 - n_steps * ends, 1 - now))
 
     def in_start(t, c):
         slot, rows, ex = lax.rem(c, IN_SLOTS), chunk(c), lax.rem(t, n_ex)
@@ -132,7 +131,7 @@
                 c = i * n_in + s
                 rows = chunk(c)
                 if load:
-                    @pl.when(c + IN_SLOTS - 1 < n_t)
+                    @pl.when((c > 0) & (c + IN_SLOTS - 1 < n_t))
                     def _():
                         in_start(task, c + IN_SLOTS - 1)
 
@@ -165,7 +164,7 @@
         ss_ref[...] = jnp.zeros_like(ss_ref)
         in_start(task, c)
 
-    rarely(is_first, begin, IN_SLOTS - 1)
+    rarely(is_first, begin, IN_SLOTS)
 
     fetch('wait', task, step, now)
     for load in (True, False):
@@ -190,6 +189,11 @@
 
         lax.fori_loop(0, n_t, put, 0)
         dx_out.start()
+
+    ends_task = (step == n_steps - 1) & (task < n_task - 1)
+    rarely(ends_task & (task + 1 >= n_ex), lambda i: tp_copy(task + 1 - n_ex).wait())
+    rarely(ends_task, lambda c: in_start(task + 1, c), IN_SLOTS)
+    pl.when(task + ends < n_task)(lambda: fetch('start', task + ends, step + 1 - n_steps * ends, 1 - now))
 
     def far_copy(axis, src, dst):
         return pltpu.make_async_remote_copy(
@@ -286,10 +290,6 @@
     def _():
         dx_out.wait()
         tp_copy(task).start()
-
-    ends_task = (step == n_steps - 1) & (task < n_task - 1)
-    rarely(ends_task & (task + 1 >= n_ex), lambda i: tp_copy(task + 1 - n_ex).wait())
-    rarely(ends_task, lambda c: in_start(task + 1, c), IN_SLOTS - 1)
 
     def finish(i):
         keep = pltpu.make_async_copy(ss_ref, ss_hbm.at[0], io_sem.at[0])

time: 1320 us -> 1320 us (level)
  no operation moved by 1% of the time
where the time goes in v1:
time: 1320 us; the launch traced here: 1310 us
  Pallas kernels  779 us (59%)
  waiting for transfers between devices  477 us (36%)
  starting transfers between devices  34.6 us (3%)
  local copies, waits for them, and re-layouts  18.4 us (1%)
    pallas_call x1, Pallas kernels, run_stack(): pl.pallas_call(functools.partial(stack_kernel, n_layers, n_ex, n_steps),...  501 us
    ppermute x18, waiting for transfers between devices, local_step(): over_y = lambda v: lax.ppermute(v, 'dp', swap_y)  340 us
    pallas_call x32, Pallas kernels, put_piece(): pl.pallas_call(put_out_kernel if transposed else put_in_kernel, out_shape...  167 us
    ppermute x18, waiting for transfers between devices, local_step(): over_x = lambda v: lax.ppermute(v, 'dp', swap_x)  136 us
    pallas_call x20, Pallas kernels, mix(): pl.pallas_call(functools.partial(mix_kernel, [at for _, _, _, at in terms...  109 us
  transfers between devices with their start and end apart: 36, of which 14 were waited for; matrix products, arithmetic and copies ran while one was open for 0% of the time, Pallas kernels for 19%

profile of v1, /device:TPU:0, one launch (start us, length us, event | category | flops | bytes accessed | tf_op | source)
XLA Modules:
  0.0 1313.4 jit_solution(831185698609433515)
XLA Ops:
  0.7 501.5 %stack.311 = (bf16[4,2048,1408]{2,1,0:T(8,128)(2,1)}, bf16[4,2048,1408]{2,1,0:T(8,128)(2,1)}, bf16[2,2048,1408]{2,1,0:T(8,128)(2,1)}, f32[4,704,3072]{2,1,0:T(8,...) custom-call(bf16[3,2,2048,3072]{3,2,1,0:T(8,128)(2,1)} %u_hbm.1, ...), custom_call_target="tpu_custom_call" | custom-call | flops 389768282112 | bytes 500000000 | tf_op jit(solution)/shard_map/stack/pallas_call | solution.py:351
  505.3 4.8 mix.20
  514.0 4.8 mix.22
  522.8 7.4 mix.24
  530.8 7.5 mix.25
  539.8 7.5 mix.26
  548.7 7.5 mix.27
  563.8 85.3 %collective-permute-done.5 = bf16[1408,384]{1,0:T(8,128)(2,1)S(1)} collective-permute-done((bf16[1408,384]{1,0:T(8,128)(2,1)S(1)}, bf16[1408,384]{1,0:T(8,128)(2,1)S(1)}, u32[]{:S(2)}, u32[]{:S(2)}) %collective-permute-start.5) | collective-permute-done | bytes 1081376 | tf_op jit(solution)/shard_map/ppermute | solution.py:492
  658.1 5.0 mix.30
  672.6 6.5 mix.32.piece_ref
  679.1 7.3 mix.33.piece_ref
  686.5 7.1 mix.34.piece_ref
  693.5 8.7 mix.35.piece_ref
  714.5 8.1 collective-permute-done.8
  727.5 18.1 %collective-permute-done.11 = bf16[352,1536]{1,0:T(8,128)(2,1)S(1)} collective-permute-done((bf16[352,1536]{1,0:T(8,128)(2,1)}, bf16[352,1536]{1,0:T(8,128)(2,1)S(1)}, u32[]{:S(2)}, u32[]{:S(2)}) %collective-permute-start.11) | collective-permute-done | bytes 1081376 | tf_op jit(solution)/shard_map/ppermute | solution.py:493
  747.6 9.4 collective-permute-done.26.piece_ref
  757.4 11.3 collective-permute-done.33.piece_ref
  770.2 10.0 collective-permute-done.24.piece_ref
  785.0 6.9 collective-permute-done.32.piece_ref
  794.4 20.9 %collective-permute-done.14.piece_ref = bf16[352,1536]{1,0:T(8,128)(2,1)} collective-permute-done((bf16[352,1536]{1,0:T(8,128)(2,1)S(1)}, bf16[352,1536]{1,0:T(8,128)(2,1)}, u32[]{:S(2)}, u32[]{:S(2)}) %collective-permute-start.14) | collective-permute-done | bytes 1081376 | tf_op jit(solution)/shard_map/ppermute | solution.py:493
  819.2 63.9 %collective-permute-done.12.piece_ref = bf16[352,1536]{1,0:T(8,128)(2,1)} collective-permute-done((bf16[352,1536]{1,0:T(8,128)(2,1)S(1)}, bf16[352,1536]{1,0:T(8,128)(2,1)}, u32[]{:S(2)}, u32[]{:S(2)}) %collective-permute-start.12) | collective-permute-done | bytes 1081376 | tf_op jit(solution)/shard_map/ppermute | solution.py:493
  884.5 31.3 %collective-permute-done.20.piece_ref = bf16[352,1536]{1,0:T(8,128)(2,1)S(1)} collective-permute-done((bf16[352,1536]{1,0:T(8,128)(2,1)S(1)}, bf16[352,1536]{1,0:T(8,128)(2,1)S(1)}, u32[]{:S(2)}, u32[]{:S(2)}) %collective-permute-start.20) | collective-permute-done | bytes 1081376 | tf_op jit(solution)/shard_map/ppermute | solution.py:492
  922.2 10.8 collective-permute-done.34.piece_ref
  934.8 111.6 %collective-permute-done.27.piece_ref = bf16[1408,384]{1,0:T(8,128)(2,1)S(1)} collective-permute-done((bf16[1408,384]{1,0:T(8,128)(2,1)S(1)}, bf16[1408,384]{1,0:T(8,128)(2,1)S(1)}, u32[]{:S(2)}, u32[]{:S(2)}) %collective-permute-start.27) | collective-permute-done | bytes 1081376 | tf_op jit(solution)/shard_map/ppermute | solution.py:493
  1054.7 42.9 %collective-permute-done.31.piece_ref = bf16[1408,768]{1,0:T(8,128)(2,1)} collective-permute-done((bf16[1408,768]{1,0:T(8,128)(2,1)}, bf16[1408,768]{1,0:T(8,128)(2,1)}, u32[]{:S(2)}, u32[]{:S(2)}) %collective-permute-start.31) | collective-permute-done | bytes 2162720 | tf_op jit(solution)/shard_map/ppermute | solution.py:493
  1098.0 46.0 %collective-permute-done.29.piece_ref = bf16[1408,768]{1,0:T(8,128)(2,1)} collective-permute-done((bf16[1408,768]{1,0:T(8,128)(2,1)}, bf16[1408,768]{1,0:T(8,128)(2,1)}, u32[]{:S(2)}, u32[]{:S(2)}) %collective-permute-start.29) | collective-permute-done | bytes 2162720 | tf_op jit(solution)/shard_map/ppermute | solution.py:493
  1146.7 7.3 put_out.16.rest_0_
  1154.0 7.3 put_out.17.rest_0_
  1165.9 4.6 put_out.19.rest_0_
  1175.1 5.2 put_in.17.rest_0_
  1187.1 7.8 put_out.20.rest_0_
  1194.9 7.3 put_out.21.rest_0_
  1202.2 7.8 put_out.22.rest_0_
  1209.9 7.3 put_out.23.rest_0_
  1217.2 4.6 put_out.24.rest_0_
  1221.9 4.6 put_out.25.rest_0_
  1226.5 4.8 put_out.26.rest_0_
  1231.3 5.2 put_in.20.rest_0_
  1236.5 5.2 put_in.21.rest_0_
  1241.7 5.2 put_in.22.rest_0_
  1246.9 5.2 put_in.23.rest_0_
  1262.8 4.6 put_out.27.rest_0_
  1270.8 7.7 put_out.28.rest_0_
  1278.5 7.7 put_out.29.rest_0_
  1286.2 4.6 put_out.30.rest_0_
  1290.8 4.8 put_out.31
  1295.6 5.2 put_in.28.rest_0_
  1300.8 5.2 put_in.29.rest_0_
  (186 shorter events, 129.8 us)
Async XLA Ops:
  530.3 124.4 %collective-permute-start = (bf16[1408,768]{1,0:T(8,128)(2,1)}, bf16[1408,768]{1,0:T(8,128)(2,1)S(1)}, u32[]{:S(2)}, u32[]{:S(2)}) collective-permute-start(bf16[1408,768]{1,0:T(8,128)(2,1)} %mix.24), channel_id=1, source_target_pairs={{0,2},{2,0},{4,6},{6,4},{1,3},{3,1},{5,7},{7,5}} | collective-permute-start | bytes 6488072 | tf_op jit(solution)/shard_map/ppermute | solution.py:492
  538.3 117.0 %collective-permute-start.1 = (bf16[352,3072]{1,0:T(8,128)(2,1)}, bf16[352,3072]{1,0:T(8,128)(2,1)}, u32[]{:S(2)}, u32[]{:S(2)}) collective-permute-start(bf16[352,3072]{1,0:T(8,128)(2,1)} %mix.25), channel_id=1, source_target_pairs={{0,4},{2,6},{4,0},{6,2},{1,5},{3,7},{5,1},{7,3}} | collective-permute-start | bytes 6488072 | tf_op jit(solution)/shard_map/ppermute | solution.py:493
  547.3 115.8 %collective-permute-start.2 = (bf16[1408,768]{1,0:T(8,128)(2,1)}, bf16[1408,768]{1,0:T(8,128)(2,1)}, u32[]{:S(2)}, u32[]{:S(2)}) collective-permute-start(bf16[1408,768]{1,0:T(8,128)(2,1)} %mix.26), channel_id=1, source_target_pairs={{0,2},{2,0},{4,6},{6,4},{1,3},{3,1},{5,7},{7,5}} | collective-permute-start | bytes 6488072 | tf_op jit(solution)/shard_map/ppermute | solution.py:492
  556.2 108.5 %collective-permute-start.3 = (bf16[352,3072]{1,0:T(8,128)(2,1)}, bf16[352,3072]{1,0:T(8,128)(2,1)}, u32[]{:S(2)}, u32[]{:S(2)}) collective-permute-start(bf16[352,3072]{1,0:T(8,128)(2,1)} %mix.27), channel_id=1, source_target_pairs={{0,4},{2,6},{4,0},{6,2},{1,5},{3,7},{5,1},{7,3}} | collective-permute-start | bytes 6488072 | tf_op jit(solution)/shard_map/ppermute | solution.py:493
  556.9 93.7 %slice-start = ((s8[4325376]{0:T(1024)(128)(4,1)}), s8[4194304]{0:T(1024)(128)(4,1)S(1)}, s32[]{:S(2)}) async-start(s8[4325376]{0:T(1024)(128)(4,1)} %bitcast.34), calls=%async_computation | async-start | bytes 8388608
  559.2 91.3 %slice-start.1 = ((s8[4325376]{0:T(1024)(128)(4,1)}), s8[131072]{0:T(1024)(128)(4,1)S(1)}, s32[]{:S(2)}) async-start(s8[4325376]{0:T(1024)(128)(4,1)} %bitcast.34), calls=%async_computation.1 | async-start | bytes 262144
  563.3 85.8 %collective-permute-start.5 = (bf16[1408,384]{1,0:T(8,128)(2,1)S(1)}, bf16[1408,384]{1,0:T(8,128)(2,1)S(1)}, u32[]{:S(2)}, u32[]{:S(2)}) collective-permute-start(bf16[1408,384]{1,0:T(8,128)(2,1)S(1)} %mix.28), channel_id=1, source_target_pairs={{0,2},{2,0},{4,6},{6,4},{1,3},{3,1},{5,7},{7,5}} | collective-permute-start | bytes 3244040 | tf_op jit(solution)/shard_map/ppermute | solution.py:492
  649.1 53.2 %collective-permute-start.4 = (bf16[1408,384]{1,0:T(8,128)(2,1)}, bf16[1408,384]{1,0:T(8,128)(2,1)}, u32[]{:S(2)}, u32[]{:S(2)}) collective-permute-start(bf16[1408,384]{1,0:T(8,128)(2,1)} %mix.20), channel_id=1, source_target_pairs={{0,4},{2,6},{4,0},{6,2},{1,5},{3,7},{5,1},{7,3}} | collective-permute-start | bytes 3244040 | tf_op jit(solution)/shard_map/ppermute | solution.py:493
  654.7 52.4 %collective-permute-start.7 = (bf16[352,1536]{1,0:T(8,128)(2,1)}, bf16[352,1536]{1,0:T(8,128)(2,1)}, u32[]{:S(2)}, u32[]{:S(2)}) collective-permute-start(bf16[352,1536]{1,0:T(8,128)(2,1)} %mix.29), channel_id=1, source_target_pairs={{0,4},{2,6},{4,0},{6,2},{1,5},{3,7},{5,1},{7,3}} | collective-permute-start | bytes 3244040 | tf_op jit(solution)/shard_map/ppermute | solution.py:493
  655.3 52.2 %collective-permute-start.6 = (bf16[352,1536]{1,0:T(8,128)(2,1)}, bf16[352,1536]{1,0:T(8,128)(2,1)}, u32[]{:S(2)}, u32[]{:S(2)}) collective-permute-start(bf16[352,1536]{1,0:T(8,128)(2,1)} %mix.21), channel_id=1, source_target_pairs={{0,2},{2,0},{4,6},{6,4},{1,3},{3,1},{5,7},{7,5}} | collective-permute-start | bytes 3244040 | tf_op jit(solution)/shard_map/ppermute | solution.py:492
  663.1 49.9 %collective-permute-start.9 = (bf16[1408,384]{1,0:T(8,128)(2,1)}, bf16[1408,384]{1,0:T(8,128)(2,1)}, u32[]{:S(2)}, u32[]{:S(2)}) collective-permute-start(bf16[1408,384]{1,0:T(8,128)(2,1)} %mix.30), channel_id=1, source_target_pairs={{0,2},{2,0},{4,6},{6,4},{1,3},{3,1},{5,7},{7,5}} | collective-permute-start | bytes 3244040 | tf_op jit(solution)/shard_map/ppermute | solution.py:492
  664.7 57.9 %collective-permute-start.8 = (bf16[1408,384]{1,0:T(8,128)(2,1)}, bf16[1408,384]{1,0:T(8,128)(2,1)}, u32[]{:S(2)}, u32[]{:S(2)}) collective-permute-start(bf16[1408,384]{1,0:T(8,128)(2,1)} %mix.22), channel_id=1, source_target_pairs={{0,4},{2,6},{4,0},{6,2},{1,5},{3,7},{5,1},{7,3}} | collective-permute-start | bytes 3244040 | tf_op jit(solution)/shard_map/ppermute | solution.py:493
  679.1 101.1 %copy-start.3 = (bf16[1408,768]{1,0:T(8,128)(2,1)}, bf16[1408,768]{1,0:T(8,128)(2,1)S(1)}, u32[]{:S(2)}) copy-start(bf16[1408,768]{1,0:T(8,128)(2,1)S(1)} %mix.32.piece_ref) | copy-start | bytes 6488068
  693.5 189.5 %copy-start.5 = (bf16[1408,768]{1,0:T(8,128)(2,1)}, bf16[1408,768]{1,0:T(8,128)(2,1)S(1)}, u32[]{:S(2)}) copy-start(bf16[1408,768]{1,0:T(8,128)(2,1)S(1)} %mix.34.piece_ref) | copy-start | bytes 6488068
  693.5 9.3 copy-start.30
  702.3 43.3 %collective-permute-start.11 = (bf16[352,1536]{1,0:T(8,128)(2,1)}, bf16[352,1536]{1,0:T(8,128)(2,1)S(1)}, u32[]{:S(2)}, u32[]{:S(2)}) collective-permute-start(bf16[352,1536]{1,0:T(8,128)(2,1)} %mix.31), channel_id=1, source_target_pairs={{0,4},{2,6},{4,0},{6,2},{1,5},{3,7},{5,1},{7,3}} | collective-permute-start | bytes 3244040 | tf_op jit(solution)/shard_map/ppermute | solution.py:493
  707.1 40.0 %collective-permute-start.10 = (bf16[352,1536]{1,0:T(8,128)(2,1)S(1)}, bf16[352,1536]{1,0:T(8,128)(2,1)S(1)}, u32[]{:S(2)}, u32[]{:S(2)}) collective-permute-start(bf16[352,1536]{1,0:T(8,128)(2,1)S(1)} %copy-done.32), channel_id=1, source_target_pairs={{0,2},{2,0},{4,6},{6,4},{1,3},{3,1},{5,7},{7,5}} | collective-permute-start | bytes 3244040 | tf_op jit(solution)/shard_map/ppermute | solution.py:492
  707.5 49.5 %collective-permute-start.26 = (bf16[1408,384]{1,0:T(8,128)(2,1)S(1)}, bf16[1408,384]{1,0:T(8,128)(2,1)S(1)}, u32[]{:S(2)}, u32[]{:S(2)}) collective-permute-start(bf16[1408,384]{1,0:T(8,128)(2,1)S(1)} %mix.36.piece_ref), channel_id=1, source_target_pairs={{0,2},{2,0},{4,6},{6,4},{1,3},{3,1},{5,7},{7,5}} | collective-permute-start | bytes 3244040 | tf_op jit(solution)/shard_map/ppermute | solution.py:492
  713.0 44.0 %copy-start.7 = (bf16[352,1536]{1,0:T(8,128)(2,1)}, bf16[352,1536]{1,0:T(8,128)(2,1)S(1)}, u32[]{:S(2)}) copy-start(bf16[352,1536]{1,0:T(8,128)(2,1)S(1)} %mix.37.piece_ref) | copy-start | bytes 3244036
  713.0 55.8 %collective-permute-start.33 = (bf16[1408,384]{1,0:T(8,128)(2,1)S(1)}, bf16[1408,384]{1,0:T(8,128)(2,1)S(1)}, u32[]{:S(2)}, u32[]{:S(2)}) collective-permute-start(bf16[1408,384]{1,0:T(8,128)(2,1)S(1)} %mix.36.piece_ref), channel_id=1, source_target_pairs={{0,4},{2,6},{4,0},{6,2},{1,5},{3,7},{5,1},{7,3}} | collective-permute-start | bytes 3244040 | tf_op jit(solution)/shard_map/ppermute | solution.py:493
  727.0 58.0 %copy-start.9 = (bf16[1408,384]{1,0:T(8,128)(2,1)}, bf16[1408,384]{1,0:T(8,128)(2,1)S(1)}, u32[]{:S(2)}) copy-start(bf16[1408,384]{1,0:T(8,128)(2,1)S(1)} %mix.38.piece_ref) | copy-start | bytes 3244036
  727.0 53.3 %collective-permute-start.24 = (bf16[1408,384]{1,0:T(8,128)(2,1)S(1)}, bf16[1408,384]{1,0:T(8,128)(2,1)}, u32[]{:S(2)}, u32[]{:S(2)}) collective-permute-start(bf16[1408,384]{1,0:T(8,128)(2,1)S(1)} %mix.38.piece_ref), channel_id=1, source_target_pairs={{0,2},{2,0},{4,6},{6,4},{1,3},{3,1},{5,7},{7,5}} | collective-permute-start | bytes 3244040 | tf_op jit(solution)/shard_map/ppermute | solution.py:492
  745.6 46.3 %collective-permute-start.32 = (bf16[1408,384]{1,0:T(8,128)(2,1)S(1)}, bf16[1408,384]{1,0:T(8,128)(2,1)S(1)}, u32[]{:S(2)}, u32[]{:S(2)}) collective-permute-start(bf16[1408,384]{1,0:T(8,128)(2,1)S(1)} %mix.38.piece_ref), channel_id=1, source_target_pairs={{0,4},{2,6},{4,0},{6,2},{1,5},{3,7},{5,1},{7,3}} | collective-permute-start | bytes 3244040 | tf_op jit(solution)/shard_map/ppermute | solution.py:493
  747.0 68.2 %collective-permute-start.14 = (bf16[352,1536]{1,0:T(8,128)(2,1)S(1)}, bf16[352,1536]{1,0:T(8,128)(2,1)}, u32[]{:S(2)}, u32[]{:S(2)}) collective-permute-start(bf16[352,1536]{1,0:T(8,128)(2,1)S(1)} %mix.37.piece_ref), channel_id=1, source_target_pairs={{0,4},{2,6},{4,0},{6,2},{1,5},{3,7},{5,1},{7,3}} | collective-permute-start | bytes 3244040 | tf_op jit(solution)/shard_map/ppermute | solution.py:493
  757.0 163.6 %copy-start.17 = (bf16[1408,384]{1,0:T(8,128)(2,1)}, bf16[1408,384]{1,0:T(8,128)(2,1)S(1)}, u32[]{:S(2)}) copy-start(bf16[1408,384]{1,0:T(8,128)(2,1)S(1)} %collective-permute-done.26.piece_ref) | copy-start | bytes 3244036
  757.0 58.7 %collective-permute-start.21 = (bf16[352,1536]{1,0:T(8,128)(2,1)S(1)}, bf16[352,1536]{1,0:T(8,128)(2,1)S(1)}, u32[]{:S(2)}, u32[]{:S(2)}) collective-permute-start(bf16[352,1536]{1,0:T(8,128)(2,1)S(1)} %mix.37.piece_ref), channel_id=1, source_target_pairs={{0,2},{2,0},{4,6},{6,4},{1,3},{3,1},{5,7},{7,5}} | collective-permute-start | bytes 3244040 | tf_op jit(solution)/shard_map/ppermute | solution.py:492
  769.8 148.5 %collective-permute-start.30 = (bf16[1408,768]{1,0:T(8,128)(2,1)S(1)}, bf16[1408,768]{1,0:T(8,128)(2,1)}, u32[]{:S(2)}, u32[]{:S(2)}) collective-permute-start(bf16[1408,768]{1,0:T(8,128)(2,1)S(1)} %mix.32.piece_ref), channel_id=1, source_target_pairs={{0,2},{2,0},{4,6},{6,4},{1,3},{3,1},{5,7},{7,5}} | collective-permute-start | bytes 6488072 | tf_op jit(solution)/shard_map/ppermute | solution.py:492
  780.3 138.5 %collective-permute-start.35 = (bf16[1408,768]{1,0:T(8,128)(2,1)S(1)}, bf16[1408,768]{1,0:T(8,128)(2,1)S(1)}, u32[]{:S(2)}, u32[]{:S(2)}) collective-permute-start(bf16[1408,768]{1,0:T(8,128)(2,1)S(1)} %mix.32.piece_ref), channel_id=1, source_target_pairs={{0,4},{2,6},{4,0},{6,2},{1,5},{3,7},{5,1},{7,3}} | collective-permute-start | bytes 6488072 | tf_op jit(solution)/shard_map/ppermute | solution.py:493
  792.9 90.2 %collective-permute-start.12 = (bf16[352,1536]{1,0:T(8,128)(2,1)S(1)}, bf16[352,1536]{1,0:T(8,128)(2,1)}, u32[]{:S(2)}, u32[]{:S(2)}) collective-permute-start(bf16[352,1536]{1,0:T(8,128)(2,1)S(1)} %mix.39.piece_ref), channel_id=1, source_target_pairs={{0,4},{2,6},{4,0},{6,2},{1,5},{3,7},{5,1},{7,3}} | collective-permute-start | bytes 3244040 | tf_op jit(solution)/shard_map/ppermute | solution.py:493
  815.2 105.4 %collective-permute-start.28 = (bf16[1408,768]{1,0:T(8,128)(2,1)S(1)}, bf16[1408,768]{1,0:T(8,128)(2,1)}, u32[]{:S(2)}, u32[]{:S(2)}) collective-permute-start(bf16[1408,768]{1,0:T(8,128)(2,1)S(1)} %mix.34.piece_ref), channel_id=1, source_target_pairs={{0,2},{2,0},{4,6},{6,4},{1,3},{3,1},{5,7},{7,5}} | collective-permute-start | bytes 6488072 | tf_op jit(solution)/shard_map/ppermute | solution.py:492
  816.7 99.2 %collective-permute-start.20 = (bf16[352,1536]{1,0:T(8,128)(2,1)S(1)}, bf16[352,1536]{1,0:T(8,128)(2,1)S(1)}, u32[]{:S(2)}, u32[]{:S(2)}) collective-permute-start(bf16[352,1536]{1,0:T(8,128)(2,1)S(1)} %mix.39.piece_ref), channel_id=1, source_target_pairs={{0,2},{2,0},{4,6},{6,4},{1,3},{3,1},{5,7},{7,5}} | collective-permute-start | bytes 3244040 | tf_op jit(solution)/shard_map/ppermute | solution.py:492
  883.1 49.9 %collective-permute-start.34 = (bf16[1408,768]{1,0:T(8,128)(2,1)S(1)}, bf16[1408,768]{1,0:T(8,128)(2,1)S(1)}, u32[]{:S(2)}, u32[]{:S(2)}) collective-permute-start(bf16[1408,768]{1,0:T(8,128)(2,1)S(1)} %mix.34.piece_ref), channel_id=1, source_target_pairs={{0,4},{2,6},{4,0},{6,2},{1,5},{3,7},{5,1},{7,3}} | collective-permute-start | bytes 6488072 | tf_op jit(solution)/shard_map/ppermute | solution.py:493
  916.8 132.0 %collective-permute-start.18 = (bf16[352,3072]{1,0:T(8,128)(2,1)S(1)}, bf16[352,3072]{1,0:T(8,128)(2,1)}, u32[]{:S(2)}, u32[]{:S(2)}) collective-permute-start(bf16[352,3072]{1,0:T(8,128)(2,1)S(1)} %mix.33.piece_ref), channel_id=1, source_target_pairs={{0,4},{2,6},{4,0},{6,2},{1,5},{3,7},{5,1},{7,3}} | collective-permute-start | bytes 6488072 | tf_op jit(solution)/shard_map/ppermute | solution.py:493
  918.3 131.5 %collective-permute-start.23 = (bf16[352,3072]{1,0:T(8,128)(2,1)S(1)}, bf16[352,3072]{1,0:T(8,128)(2,1)}, u32[]{:S(2)}, u32[]{:S(2)}) collective-permute-start(bf16[352,3072]{1,0:T(8,128)(2,1)S(1)} %mix.33.piece_ref), channel_id=1, source_target_pairs={{0,2},{2,0},{4,6},{6,4},{1,3},{3,1},{5,7},{7,5}} | collective-permute-start | bytes 6488072 | tf_op jit(solution)/shard_map/ppermute | solution.py:492
  920.2 130.0 %collective-permute-start.16 = (bf16[352,3072]{1,0:T(8,128)(2,1)}, bf16[352,3072]{1,0:T(8,128)(2,1)}, u32[]{:S(2)}, u32[]{:S(2)}) collective-permute-start(bf16[352,3072]{1,0:T(8,128)(2,1)} %mix.35.piece_ref), channel_id=1, source_target_pairs={{0,4},{2,6},{4,0},{6,2},{1,5},{3,7},{5,1},{7,3}} | collective-permute-start | bytes 6488072 | tf_op jit(solution)/shard_map/ppermute | solution.py:493
  920.6 125.7 %collective-permute-start.27 = (bf16[1408,384]{1,0:T(8,128)(2,1)S(1)}, bf16[1408,384]{1,0:T(8,128)(2,1)S(1)}, u32[]{:S(2)}, u32[]{:S(2)}) collective-permute-start(bf16[1408,384]{1,0:T(8,128)(2,1)S(1)} %collective-permute-done.26.piece_ref), channel_id=1, source_target_pairs={{0,4},{2,6},{4,0},{6,2},{1,5},{3,7},{5,1},{7,3}} | collective-permute-start | bytes 3244040 | tf_op jit(solution)/shard_map/ppermute | solution.py:493
  934.4 118.9 %collective-permute-start.22 = (bf16[352,3072]{1,0:T(8,128)(2,1)}, bf16[352,3072]{1,0:T(8,128)(2,1)}, u32[]{:S(2)}, u32[]{:S(2)}) collective-permute-start(bf16[352,3072]{1,0:T(8,128)(2,1)} %mix.35.piece_ref), channel_id=1, source_target_pairs={{0,2},{2,0},{4,6},{6,4},{1,3},{3,1},{5,7},{7,5}} | collective-permute-start | bytes 6488072 | tf_op jit(solution)/shard_map/ppermute | solution.py:492
  1047.4 50.2 %collective-permute-start.31 = (bf16[1408,768]{1,0:T(8,128)(2,1)}, bf16[1408,768]{1,0:T(8,128)(2,1)}, u32[]{:S(2)}, u32[]{:S(2)}) collective-permute-start(bf16[1408,768]{1,0:T(8,128)(2,1)} %collective-permute-done.30.piece_ref), channel_id=1, source_target_pairs={{0,4},{2,6},{4,0},{6,2},{1,5},{3,7},{5,1},{7,3}} | collective-permute-start | bytes 6488072 | tf_op jit(solution)/shard_map/ppermute | solution.py:493
  1048.8 95.1 %collective-permute-start.29 = (bf16[1408,768]{1,0:T(8,128)(2,1)}, bf16[1408,768]{1,0:T(8,128)(2,1)}, u32[]{:S(2)}, u32[]{:S(2)}) collective-permute-start(bf16[1408,768]{1,0:T(8,128)(2,1)} %collective-permute-done.28.piece_ref), channel_id=1, source_target_pairs={{0,4},{2,6},{4,0},{6,2},{1,5},{3,7},{5,1},{7,3}} | collective-permute-start | bytes 6488072 | tf_op jit(solution)/shard_map/ppermute | solution.py:493
  1049.8 245.8 %collective-permute-start.19 = (bf16[352,3072]{1,0:T(8,128)(2,1)}, bf16[352,3072]{1,0:T(8,128)(2,1)}, u32[]{:S(2)}, u32[]{:S(2)}) collective-permute-start(bf16[352,3072]{1,0:T(8,128)(2,1)} %collective-permute-done.18.piece_ref), channel_id=1, source_target_pairs={{0,2},{2,0},{4,6},{6,4},{1,3},{3,1},{5,7},{7,5}} | collective-permute-start | bytes 6488072 | tf_op jit(solution)/shard_map/ppermute | solution.py:492
  1050.2 250.7 %collective-permute-start.17 = (bf16[352,3072]{1,0:T(8,128)(2,1)}, bf16[352,3072]{1,0:T(8,128)(2,1)}, u32[]{:S(2)}, u32[]{:S(2)}) collective-permute-start(bf16[352,3072]{1,0:T(8,128)(2,1)} %collective-permute-done.16.piece_ref), channel_id=1, source_target_pairs={{0,2},{2,0},{4,6},{6,4},{1,3},{3,1},{5,7},{7,5}} | collective-permute-start | bytes 6488072 | tf_op jit(solution)/shard_map/ppermute | solution.py:492
  1053.3 237.6 %collective-permute-start.25 = (bf16[1408,384]{1,0:T(8,128)(2,1)}, bf16[1408,384]{1,0:T(8,128)(2,1)}, u32[]{:S(2)}, u32[]{:S(2)}) collective-permute-start(bf16[1408,384]{1,0:T(8,128)(2,1)} %collective-permute-done.24.piece_ref), channel_id=1, source_target_pairs={{0,4},{2,6},{4,0},{6,2},{1,5},{3,7},{5,1},{7,3}} | collective-permute-start | bytes 3244040 | tf_op jit(solution)/shard_map/ppermute | solution.py:493
  1097.6 208.4 %collective-permute-start.15 = (bf16[352,1536]{1,0:T(8,128)(2,1)}, bf16[352,1536]{1,0:T(8,128)(2,1)}, u32[]{:S(2)}, u32[]{:S(2)}) collective-permute-start(bf16[352,1536]{1,0:T(8,128)(2,1)} %collective-permute-done.14.piece_ref), channel_id=1, source_target_pairs={{0,2},{2,0},{4,6},{6,4},{1,3},{3,1},{5,7},{7,5}} | collective-permute-start | bytes 3244040 | tf_op jit(solution)/shard_map/ppermute | solution.py:492
  1144.0 165.7 %collective-permute-start.13 = (bf16[352,1536]{1,0:T(8,128)(2,1)}, bf16[352,1536]{1,0:T(8,128)(2,1)}, u32[]{:S(2)}, u32[]{:S(2)}) collective-permute-start(bf16[352,1536]{1,0:T(8,128)(2,1)} %collective-permute-done.12.piece_ref), channel_id=1, source_target_pairs={{0,2},{2,0},{4,6},{6,4},{1,3},{3,1},{5,7},{7,5}} | collective-permute-start | bytes 3244040 | tf_op jit(solution)/shard_map/ppermute | solution.py:492
  1146.7 7.3 copy-start.6
  1187.1 7.8 copy-start.14
  1202.1 7.8 copy-start.16
  1278.5 7.7 copy-start.28
  (23 other events, 64.9 us)

commit v2 on v1

--- a/solution.py
+++ b/solution.py
@@ -11,12 +11,14 @@
 INV_SQRT2 = 0.7071067811865476
 INV_SQRT_2PI = 0.3989422804014327
 LOG2_E = 1.4426950408889634
+F32_MAX = 3.4028234663852886e38
 F_BLOCK = 512
 T_CHUNK = 256
 IN_SLOTS = 4
 LOAD_CHUNKS = 2
 MIX_ROWS = 32
-N_SUM, N_FIRST, N_PUT = 20, 12, 32
+N_PARTS = 3
+N_SUM, N_FIRST, N_PUT = 8 + 6 * N_PARTS, 4 + 4 * N_PARTS, 16 + 8 * N_PARTS
 VMEM_LIMIT = 67_000_000
 
 F32 = jnp.float32
@@ -188,12 +190,12 @@
             return carry
 
         lax.fori_loop(0, n_t, put, 0)
-        dx_out.start()
-
+
+    pl.when(task + ends < n_task)(lambda: fetch('start', task + ends, step + 1 - n_steps * ends, 1 - now))
     ends_task = (step == n_steps - 1) & (task < n_task - 1)
     rarely(ends_task & (task + 1 >= n_ex), lambda i: tp_copy(task + 1 - n_ex).wait())
     rarely(ends_task, lambda c: in_start(task + 1, c), IN_SLOTS)
-    pl.when(task + ends < n_task)(lambda: fetch('start', task + ends, step + 1 - n_steps * ends, 1 - now))
+    pl.when(ends_early)(dx_out.start)
 
     def far_copy(axis, src, dst):
         return pltpu.make_async_remote_copy(
@@ -361,20 +363,24 @@
     )(pre_act, w_in, w_out, block_in, d_out)
 
 
-def norm_kernel(sq_ref, out_ref):
+def clip_kernel(norm_ref, sq_ref, out_ref):
+    limit = norm_ref[0]
     for d in range(out_ref.shape[0]):
         for ex in range(out_ref.shape[1]):
-            out_ref[d, ex] = jnp.sum(sq_ref[2 * d, ex] + sq_ref[2 * d + 1, ex])
-
-
-def chip_norms(squares):
+            sq = jnp.sum(sq_ref[2 * d, ex] + sq_ref[2 * d + 1, ex], keepdims=True)
+            root = jnp.sqrt(sq)
+            factor = jnp.where(root > limit, limit / root, 1.0)
+            out_ref[d, ex] = jnp.where(sq > F32_MAX, 0.0, factor)[0, 0]
+
+
+def clip_factors(squares, clip_norm):
     return pl.pallas_call(
-        norm_kernel,
+        clip_kernel,
         out_shape=jax.ShapeDtypeStruct((3, squares.shape[1]), F32),
-        in_specs=[pl.BlockSpec(memory_space=pltpu.VMEM)],
+        in_specs=[pl.BlockSpec(memory_space=pltpu.SMEM), pl.BlockSpec(memory_space=pltpu.VMEM)],
         out_specs=pl.BlockSpec(memory_space=pltpu.SMEM),
-        name='norms',
-    )(squares)
+        name='clip',
+    )(clip_norm.reshape(1), squares)
 
 
 def mix_kernel(factors, sc_ref, clip_ref, *refs):
@@ -395,8 +401,8 @@
 def mix(which, shape, terms, clip, before, part, n_parts):
     rows, width = shape
     part_width = width // n_parts
-    block = (rows, width // 4) if which == 0 else (rows // 4, part_width)
-    n_blocks = 4 // n_parts if which == 0 else 4
+    n_blocks = 4 if n_parts == 1 else 2
+    block = (rows, part_width // n_blocks) if which == 0 else (rows // n_blocks, part_width)
 
     def spec(k, v, lead):
         off = part * n_blocks if which == 0 and v.shape[2] > part_width else 0
@@ -450,7 +456,7 @@
 def put_piece(transposed, total, layer, quarter, part, coef, piece, noise):
     if transposed:
         rows, width = piece.shape[1], piece.shape[0]
-        block = 256 if rows % 256 == 0 else 128
+        block = 256 if rows > 512 else 128
         first = part * (rows // block)
         piece_spec = pl.BlockSpec((width, block), lambda i, sc: (0, i))
         big_spec = pl.BlockSpec((1, 1, block, width), lambda i, sc: (sc[0], sc[1], first + i, 0))
@@ -493,7 +499,7 @@
         over_y = lambda v: lax.ppermute(v, 'dp', swap_y)
         res = run_stack(pre_act, w_in, w_out, block_in, d_out)
         g1k, _, g1r, g2k, _, g2r, g1l, g2l, _, g1er, _, g2er, squares = res[3:]
-        clip = jnp.minimum(1.0, clip_norm / jnp.sqrt(chip_norms(squares)))
+        clip = clip_factors(squares, clip_norm)
         coef = jnp.stack([noise_mult * clip_norm, jnp.float32(1.0 / batch_total)])
 
         noise_in4 = noise_in.reshape(n_layers, 4, d_model // 4, d_ff)
@@ -528,7 +534,7 @@
                 terms += [(early_far[which], first + k, pos, (1 + which, k)) for k in range(local_batch)]
             return terms + [(v[None], 0, 0, None) for v in more]
 
-        last = [(0, part, 2) for part in range(2)]
+        last = [(0, part, N_PARTS) for part in range(N_PARTS)]
         turns = [(layer, 0, 1) for layer in range(n_layers - 1, 0, -1)] + last
         got, far_last, places = {}, {}, {}
         for _, part, n_parts in last:

time: 1320 us -> 1390 us (1.053)
  Pallas kernels: 779 us -> 797 us
  starting transfers between devices: 34.6 us -> 50 us
  waiting for transfers between devices: 477 us -> 491 us
    ppermute x18 -> x23, waiting for transfers between devices: 136 us -> 237 us  [local_step(): over_x = lambda v: lax.ppermute(v, 'dp', swap_x)]
    ppermute x18 -> x23, waiting for transfers between devices: 340 us -> 254 us  [local_step(): over_y = lambda v: lax.ppermute(v, 'dp', swap_y)]
    unnamed x70 -> x130, local copies, waits for them, and re-layouts: 18.2 us -> 30.7 us
    ppermute x18 -> x23, starting transfers between devices: 20.9 us -> 27.9 us  [local_step(): over_y = lambda v: lax.ppermute(v, 'dp', swap_y)]
    pallas_call x32 -> x40, Pallas kernels: 167 us -> 173 us  [put_piece(): pl.pallas_call(put_out_kernel if transposed else put_in_kernel, out_shape...]
    pallas_call x20 -> x26, Pallas kernels: 109 us -> 114 us  [mix(): pl.pallas_call(functools.partial(mix_kernel, [at for _, _, _, at in terms...]
  transfers between devices with their start and end apart: 36 -> 46, of which waited for: 14 -> 23; matrix products, arithmetic and copies ran while one was open for 0% -> 0% of each run, Pallas kernels for 19% -> 20%
where the time goes in v2:
time: 1390 us; the launch traced here: 1370 us
  Pallas kernels  797 us (57%)
  waiting for transfers between devices  491 us (35%)
  starting transfers between devices  50 us (4%)
  local copies, waits for them, and re-layouts  30.9 us (2%)
    pallas_call x1, Pallas kernels, run_stack(): pl.pallas_call(functools.partial(stack_kernel, n_layers, n_ex, n_steps),...  508 us
    ppermute x23, waiting for transfers between devices, local_step(): over_y = lambda v: lax.ppermute(v, 'dp', swap_y)  254 us
    ppermute x23, waiting for transfers between devices, local_step(): over_x = lambda v: lax.ppermute(v, 'dp', swap_x)  237 us
    pallas_call x40, Pallas kernels, put_piece(): pl.pallas_call(put_out_kernel if transposed else put_in_kernel, out_shape...  173 us
    pallas_call x26, Pallas kernels, mix(): pl.pallas_call(functools.partial(mix_kernel, [at for _, _, _, at in terms...  114 us
    unnamed x130, local copies, waits for them, and re-layouts  30.7 us
    ppermute x23, starting transfers between devices, local_step(): over_y = lambda v: lax.ppermute(v, 'dp', swap_y)  27.9 us
  transfers between devices with their start and end apart: 46, of which 23 were waited for; matrix products, arithmetic and copies ran while one was open for 0% of the time, Pallas kernels for 20%

profile of v2, /device:TPU:0, one launch (start us, length us, event | category | flops | bytes accessed | tf_op | source)
XLA Modules:
  0.0 1374.2 jit_solution(6311929161557927467)
XLA Ops:
  1.4 507.6 %stack.363 = (bf16[4,2048,1408]{2,1,0:T(8,128)(2,1)}, bf16[4,2048,1408]{2,1,0:T(8,128)(2,1)}, bf16[2,2048,1408]{2,1,0:T(8,128)(2,1)}, f32[4,704,3072]{2,1,0:T(8,...) custom-call(bf16[3,2,2048,3072]{3,2,1,0:T(8,128)(2,1)} %u_hbm.1, ...), custom_call_target="tpu_custom_call" | custom-call | flops 389768282112 | bytes 500000000 | tf_op jit(solution)/shard_map/stack/pallas_call | solution.py:353
  533.6 7.5 mix.32
  541.1 7.5 mix.33
  548.6 7.5 mix.34
  556.0 6.5 mix.35
  574.8 12.1 collective-permute-done.5
  597.2 5.3 collective-permute-done.6
  603.1 106.4 %collective-permute-done.9 = bf16[1408,256]{1,0:T(8,128)(2,1)S(1)} collective-permute-done((bf16[1408,256]{1,0:T(8,128)(2,1)S(1)}, bf16[1408,256]{1,0:T(8,128)(2,1)S(1)}, u32[]{:S(2)}, u32[]{:S(2)}) %collective-permute-start.9) | collective-permute-done | bytes 720928 | tf_op jit(solution)/shard_map/ppermute | solution.py:498
  713.1 3.7 mix.39
  716.8 10.9 collective-permute-done.8
  729.5 3.5 mix.40
  733.0 3.5 mix.41
  739.6 7.1 mix.42.piece_ref
  746.7 7.3 mix.43.piece_ref
  754.0 7.0 mix.44.piece_ref
  761.1 8.6 mix.45.piece_ref
  792.8 14.3 %collective-permute-done.35.piece_ref = bf16[1408,256]{1,0:T(8,128)(2,1)S(1)} collective-permute-done((bf16[1408,256]{1,0:T(8,128)(2,1)S(1)}, bf16[1408,256]{1,0:T(8,128)(2,1)S(1)}, u32[]{:S(2)}, u32[]{:S(2)}) %collective-permute-start.35) | collective-permute-done | bytes 720928 | tf_op jit(solution)/shard_map/ppermute | solution.py:498
  810.9 11.6 collective-permute-done.33.piece_ref
  825.5 12.5 collective-permute-done.31.piece_ref
  847.2 6.3 collective-permute-done.28.piece_ref
  855.8 5.7 collective-permute-done.18.piece_ref
  863.5 51.8 %collective-permute-done.27.piece_ref = bf16[352,1024]{1,0:T(8,128)(2,1)S(1)} collective-permute-done((bf16[352,1024]{1,0:T(8,128)(2,1)S(1)}, bf16[352,1024]{1,0:T(8,128)(2,1)S(1)}, u32[]{:S(2)}, u32[]{:S(2)}) %collective-permute-start.27) | collective-permute-done | bytes 720928 | tf_op jit(solution)/shard_map/ppermute | solution.py:498
  918.5 4.8 collective-permute-done.16.piece_ref
  929.7 8.9 collective-permute-done.36.piece_ref
  940.6 13.5 collective-permute-done.34.piece_ref
  956.4 13.1 collective-permute-done.32.piece_ref
  974.9 14.6 %collective-permute-done.37.piece_ref = bf16[1408,768]{1,0:T(8,128)(2,1)} collective-permute-done((bf16[1408,768]{1,0:T(8,128)(2,1)S(1)}, bf16[1408,768]{1,0:T(8,128)(2,1)}, u32[]{:S(2)}, u32[]{:S(2)}) %collective-permute-start.37) | collective-permute-done | bytes 2162720 | tf_op jit(solution)/shard_map/ppermute | solution.py:498
  990.6 25.2 %collective-permute-done.44.piece_ref = bf16[1408,768]{1,0:T(8,128)(2,1)S(1)} collective-permute-done((bf16[1408,768]{1,0:T(8,128)(2,1)S(1)}, bf16[1408,768]{1,0:T(8,128)(2,1)S(1)}, u32[]{:S(2)}, u32[]{:S(2)}) %collective-permute-start.44) | collective-permute-done | bytes 2162720 | tf_op jit(solution)/shard_map/ppermute | solution.py:499
  1018.8 43.4 %collective-permute-done.24.piece_ref = bf16[352,3072]{1,0:T(8,128)(2,1)S(1)} collective-permute-done((bf16[352,3072]{1,0:T(8,128)(2,1)S(1)}, bf16[352,3072]{1,0:T(8,128)(2,1)S(1)}, u32[]{:S(2)}, u32[]{:S(2)}) %collective-permute-start.24) | collective-permute-done | bytes 2162720 | tf_op jit(solution)/shard_map/ppermute | solution.py:499
  1066.0 42.6 %collective-permute-done.22.piece_ref = bf16[352,3072]{1,0:T(8,128)(2,1)} collective-permute-done((bf16[352,3072]{1,0:T(8,128)(2,1)}, bf16[352,3072]{1,0:T(8,128)(2,1)}, u32[]{:S(2)}, u32[]{:S(2)}) %collective-permute-start.22) | collective-permute-done | bytes 2162720 | tf_op jit(solution)/shard_map/ppermute | solution.py:499
  1111.7 43.3 %collective-permute-done.40.piece_ref = bf16[1408,768]{1,0:T(8,128)(2,1)} collective-permute-done((bf16[1408,768]{1,0:T(8,128)(2,1)}, bf16[1408,768]{1,0:T(8,128)(2,1)}, u32[]{:S(2)}, u32[]{:S(2)}) %collective-permute-start.40) | collective-permute-done | bytes 2162720 | tf_op jit(solution)/shard_map/ppermute | solution.py:499
  1156.1 40.5 %collective-permute-done.38.piece_ref = bf16[1408,768]{1,0:T(8,128)(2,1)} collective-permute-done((bf16[1408,768]{1,0:T(8,128)(2,1)}, bf16[1408,768]{1,0:T(8,128)(2,1)}, u32[]{:S(2)}, u32[]{:S(2)}) %collective-permute-start.38) | collective-permute-done | bytes 2162720 | tf_op jit(solution)/shard_map/ppermute | solution.py:499
  1200.3 7.3 put_out.20.rest_0_
  1207.6 7.3 put_out.21.rest_0_
  1224.0 4.6 put_in.20.rest_0_
  1228.6 5.2 put_in.21.rest_0_
  1242.6 7.8 put_out.25.rest_0_
  1250.4 7.3 put_out.26.rest_0_
  1257.7 7.8 put_out.27.rest_0_
  1265.5 7.3 put_out.28.rest_0_
  1288.0 4.6 put_in.25.rest_0_
  1292.6 5.2 put_in.26.rest_0_
  1297.8 5.2 put_in.27.rest_0_
  1303.0 5.2 put_in.28.rest_0_
  1329.5 7.7 put_out.35.rest_0_
  1337.2 7.7 put_out.36.rest_0_
  1354.0 5.2 put_in.35.rest_0_
  1359.2 5.2 put_in.36.rest_0_
  (284 shorter events, 206.8 us)
Async XLA Ops:
  515.0 73.4 %collective-permute-start.4 = (bf16[1408,256]{1,0:T(8,128)(2,1)}, bf16[1408,256]{1,0:T(8,128)(2,1)}, u32[]{:S(2)}, u32[]{:S(2)}) collective-permute-start(bf16[1408,256]{1,0:T(8,128)(2,1)} %mix.26), channel_id=1, source_target_pairs={{0,4},{2,6},{4,0},{6,2},{1,5},{3,7},{5,1},{7,3}} | collective-permute-start | bytes 2162696 | tf_op jit(solution)/shard_map/ppermute | solution.py:499
  567.9 19.0 %collective-permute-start.5 = (bf16[1408,256]{1,0:T(8,128)(2,1)S(1)}, bf16[1408,256]{1,0:T(8,128)(2,1)S(1)}, u32[]{:S(2)}, u32[]{:S(2)}) collective-permute-start(bf16[1408,256]{1,0:T(8,128)(2,1)S(1)} %mix.36), channel_id=1, source_target_pairs={{0,2},{2,0},{4,6},{6,4},{1,3},{3,1},{5,7},{7,5}} | collective-permute-start | bytes 2162696 | tf_op jit(solution)/shard_map/ppermute | solution.py:498
  571.3 18.6 %collective-permute-start.7 = (bf16[352,1024]{1,0:T(8,128)(2,1)S(1)}, bf16[352,1024]{1,0:T(8,128)(2,1)S(1)}, u32[]{:S(2)}, u32[]{:S(2)}) collective-permute-start(bf16[352,1024]{1,0:T(8,128)(2,1)S(1)} %mix.37), channel_id=1, source_target_pairs={{0,4},{2,6},{4,0},{6,2},{1,5},{3,7},{5,1},{7,3}} | collective-permute-start | bytes 2162696 | tf_op jit(solution)/shard_map/ppermute | solution.py:499
  572.8 29.7 %collective-permute-start.6 = (bf16[352,1024]{1,0:T(8,128)(2,1)}, bf16[352,1024]{1,0:T(8,128)(2,1)}, u32[]{:S(2)}, u32[]{:S(2)}) collective-permute-start(bf16[352,1024]{1,0:T(8,128)(2,1)} %mix.27), channel_id=1, source_target_pairs={{0,2},{2,0},{4,6},{6,4},{1,3},{3,1},{5,7},{7,5}} | collective-permute-start | bytes 2162696 | tf_op jit(solution)/shard_map/ppermute | solution.py:498
  573.3 155.0 %collective-permute-start = (bf16[1408,768]{1,0:T(8,128)(2,1)}, bf16[1408,768]{1,0:T(8,128)(2,1)}, u32[]{:S(2)}, u32[]{:S(2)}) collective-permute-start(bf16[1408,768]{1,0:T(8,128)(2,1)} %mix.32), channel_id=1, source_target_pairs={{0,2},{2,0},{4,6},{6,4},{1,3},{3,1},{5,7},{7,5}} | collective-permute-start | bytes 6488072 | tf_op jit(solution)/shard_map/ppermute | solution.py:498
  587.8 148.7 %collective-permute-start.1 = (bf16[352,3072]{1,0:T(8,128)(2,1)}, bf16[352,3072]{1,0:T(8,128)(2,1)}, u32[]{:S(2)}, u32[]{:S(2)}) collective-permute-start(bf16[352,3072]{1,0:T(8,128)(2,1)} %mix.33), channel_id=1, source_target_pairs={{0,4},{2,6},{4,0},{6,2},{1,5},{3,7},{5,1},{7,3}} | collective-permute-start | bytes 6488072 | tf_op jit(solution)/shard_map/ppermute | solution.py:499
  588.4 149.0 %collective-permute-start.2 = (bf16[1408,768]{1,0:T(8,128)(2,1)}, bf16[1408,768]{1,0:T(8,128)(2,1)}, u32[]{:S(2)}, u32[]{:S(2)}) collective-permute-start(bf16[1408,768]{1,0:T(8,128)(2,1)} %mix.34), channel_id=1, source_target_pairs={{0,2},{2,0},{4,6},{6,4},{1,3},{3,1},{5,7},{7,5}} | collective-permute-start | bytes 6488072 | tf_op jit(solution)/shard_map/ppermute | solution.py:498
  590.8 148.1 %collective-permute-start.3 = (bf16[352,3072]{1,0:T(8,128)(2,1)S(1)}, bf16[352,3072]{1,0:T(8,128)(2,1)}, u32[]{:S(2)}, u32[]{:S(2)}) collective-permute-start(bf16[352,3072]{1,0:T(8,128)(2,1)S(1)} %mix.35), channel_id=1, source_target_pairs={{0,4},{2,6},{4,0},{6,2},{1,5},{3,7},{5,1},{7,3}} | collective-permute-start | bytes 6488072 | tf_op jit(solution)/shard_map/ppermute | solution.py:499
  594.5 135.0 %slice-start.4 = ((s8[4325376]{0:T(1024)(128)(4,1)}), s8[131072]{0:T(1024)(128)(4,1)S(1)}, s32[]{:S(2)}) async-start(s8[4325376]{0:T(1024)(128)(4,1)} %bitcast.47), calls=%async_computation.4 | async-start | bytes 262144
  602.5 107.0 %collective-permute-start.9 = (bf16[1408,256]{1,0:T(8,128)(2,1)S(1)}, bf16[1408,256]{1,0:T(8,128)(2,1)S(1)}, u32[]{:S(2)}, u32[]{:S(2)}) collective-permute-start(bf16[1408,256]{1,0:T(8,128)(2,1)S(1)} %mix.38), channel_id=1, source_target_pairs={{0,2},{2,0},{4,6},{6,4},{1,3},{3,1},{5,7},{7,5}} | collective-permute-start | bytes 2162696 | tf_op jit(solution)/shard_map/ppermute | solution.py:498
  710.3 17.4 %collective-permute-start.8 = (bf16[1408,256]{1,0:T(8,128)(2,1)}, bf16[1408,256]{1,0:T(8,128)(2,1)}, u32[]{:S(2)}, u32[]{:S(2)}) collective-permute-start(bf16[1408,256]{1,0:T(8,128)(2,1)} %copy-done.56), channel_id=1, source_target_pairs={{0,4},{2,6},{4,0},{6,2},{1,5},{3,7},{5,1},{7,3}} | collective-permute-start | bytes 2162696 | tf_op jit(solution)/shard_map/ppermute | solution.py:499
  727.7 46.1 %collective-permute-start.10 = (bf16[352,1024]{1,0:T(8,128)(2,1)}, bf16[352,1024]{1,0:T(8,128)(2,1)}, u32[]{:S(2)}, u32[]{:S(2)}) collective-permute-start(bf16[352,1024]{1,0:T(8,128)(2,1)} %copy-done.51), channel_id=1, source_target_pairs={{0,2},{2,0},{4,6},{6,4},{1,3},{3,1},{5,7},{7,5}} | collective-permute-start | bytes 2162696 | tf_op jit(solution)/shard_map/ppermute | solution.py:498
  728.3 44.3 %collective-permute-start.11 = (bf16[352,1024]{1,0:T(8,128)(2,1)}, bf16[352,1024]{1,0:T(8,128)(2,1)}, u32[]{:S(2)}, u32[]{:S(2)}) collective-permute-start(bf16[352,1024]{1,0:T(8,128)(2,1)} %mix.39), channel_id=1, source_target_pairs={{0,4},{2,6},{4,0},{6,2},{1,5},{3,7},{5,1},{7,3}} | collective-permute-start | bytes 2162696 | tf_op jit(solution)/shard_map/ppermute | solution.py:499
  736.5 44.1 %collective-permute-start.13 = (bf16[1408,256]{1,0:T(8,128)(2,1)}, bf16[1408,256]{1,0:T(8,128)(2,1)}, u32[]{:S(2)}, u32[]{:S(2)}) collective-permute-start(bf16[1408,256]{1,0:T(8,128)(2,1)} %mix.40), channel_id=1, source_target_pairs={{0,2},{2,0},{4,6},{6,4},{1,3},{3,1},{5,7},{7,5}} | collective-permute-start | bytes 2162696 | tf_op jit(solution)/shard_map/ppermute | solution.py:498
  737.4 44.6 %collective-permute-start.12 = (bf16[1408,256]{1,0:T(8,128)(2,1)}, bf16[1408,256]{1,0:T(8,128)(2,1)}, u32[]{:S(2)}, u32[]{:S(2)}) collective-permute-start(bf16[1408,256]{1,0:T(8,128)(2,1)} %mix.30), channel_id=1, source_target_pairs={{0,4},{2,6},{4,0},{6,2},{1,5},{3,7},{5,1},{7,3}} | collective-permute-start | bytes 2162696 | tf_op jit(solution)/shard_map/ppermute | solution.py:499
  738.9 43.8 %collective-permute-start.15 = (bf16[352,1024]{1,0:T(8,128)(2,1)}, bf16[352,1024]{1,0:T(8,128)(2,1)}, u32[]{:S(2)}, u32[]{:S(2)}) collective-permute-start(bf16[352,1024]{1,0:T(8,128)(2,1)} %mix.41), channel_id=1, source_target_pairs={{0,4},{2,6},{4,0},{6,2},{1,5},{3,7},{5,1},{7,3}} | collective-permute-start | bytes 2162696 | tf_op jit(solution)/shard_map/ppermute | solution.py:499
  761.1 193.0 %copy-start.5 = (bf16[1408,768]{1,0:T(8,128)(2,1)}, bf16[1408,768]{1,0:T(8,128)(2,1)S(1)}, u32[]{:S(2)}) copy-start(bf16[1408,768]{1,0:T(8,128)(2,1)S(1)} %mix.44.piece_ref) | copy-start | bytes 6488068
  772.6 19.0 %collective-permute-start.14 = (bf16[352,1024]{1,0:T(8,128)(2,1)S(1)}, bf16[352,1024]{1,0:T(8,128)(2,1)S(1)}, u32[]{:S(2)}, u32[]{:S(2)}) collective-permute-start(bf16[352,1024]{1,0:T(8,128)(2,1)S(1)} %copy-done.50), channel_id=1, source_target_pairs={{0,2},{2,0},{4,6},{6,4},{1,3},{3,1},{5,7},{7,5}} | collective-permute-start | bytes 2162696 | tf_op jit(solution)/shard_map/ppermute | solution.py:498
  773.8 33.3 %collective-permute-start.35 = (bf16[1408,256]{1,0:T(8,128)(2,1)S(1)}, bf16[1408,256]{1,0:T(8,128)(2,1)S(1)}, u32[]{:S(2)}, u32[]{:S(2)}) collective-permute-start(bf16[1408,256]{1,0:T(8,128)(2,1)S(1)} %mix.46.piece_ref), channel_id=1, source_target_pairs={{0,2},{2,0},{4,6},{6,4},{1,3},{3,1},{5,7},{7,5}} | collective-permute-start | bytes 2162696 | tf_op jit(solution)/shard_map/ppermute | solution.py:498
  780.6 28.9 %collective-permute-start.43 = (bf16[1408,256]{1,0:T(8,128)(2,1)S(1)}, bf16[1408,256]{1,0:T(8,128)(2,1)S(1)}, u32[]{:S(2)}, u32[]{:S(2)}) collective-permute-start(bf16[1408,256]{1,0:T(8,128)(2,1)S(1)} %mix.46.piece_ref), channel_id=1, source_target_pairs={{0,4},{2,6},{4,0},{6,2},{1,5},{3,7},{5,1},{7,3}} | collective-permute-start | bytes 2162696 | tf_op jit(solution)/shard_map/ppermute | solution.py:499
  782.1 40.5 %collective-permute-start.33 = (bf16[1408,256]{1,0:T(8,128)(2,1)S(1)}, bf16[1408,256]{1,0:T(8,128)(2,1)S(1)}, u32[]{:S(2)}, u32[]{:S(2)}) collective-permute-start(bf16[1408,256]{1,0:T(8,128)(2,1)S(1)} %mix.48.piece_ref), channel_id=1, source_target_pairs={{0,2},{2,0},{4,6},{6,4},{1,3},{3,1},{5,7},{7,5}} | collective-permute-start | bytes 2162696 | tf_op jit(solution)/shard_map/ppermute | solution.py:498
  782.7 41.0 %collective-permute-start.42 = (bf16[1408,256]{1,0:T(8,128)(2,1)S(1)}, bf16[1408,256]{1,0:T(8,128)(2,1)S(1)}, u32[]{:S(2)}, u32[]{:S(2)}) collective-permute-start(bf16[1408,256]{1,0:T(8,128)(2,1)S(1)} %mix.48.piece_ref), channel_id=1, source_target_pairs={{0,4},{2,6},{4,0},{6,2},{1,5},{3,7},{5,1},{7,3}} | collective-permute-start | bytes 2162696 | tf_op jit(solution)/shard_map/ppermute | solution.py:499
  791.7 46.3 %collective-permute-start.31 = (bf16[1408,256]{1,0:T(8,128)(2,1)S(1)}, bf16[1408,256]{1,0:T(8,128)(2,1)S(1)}, u32[]{:S(2)}, u32[]{:S(2)}) collective-permute-start(bf16[1408,256]{1,0:T(8,128)(2,1)S(1)} %mix.50.piece_ref), channel_id=1, source_target_pairs={{0,2},{2,0},{4,6},{6,4},{1,3},{3,1},{5,7},{7,5}} | collective-permute-start | bytes 2162696 | tf_op jit(solution)/shard_map/ppermute | solution.py:498
  807.1 32.0 %collective-permute-start.41 = (bf16[1408,256]{1,0:T(8,128)(2,1)S(1)}, bf16[1408,256]{1,0:T(8,128)(2,1)S(1)}, u32[]{:S(2)}, u32[]{:S(2)}) collective-permute-start(bf16[1408,256]{1,0:T(8,128)(2,1)S(1)} %mix.50.piece_ref), channel_id=1, source_target_pairs={{0,4},{2,6},{4,0},{6,2},{1,5},{3,7},{5,1},{7,3}} | collective-permute-start | bytes 2162696 | tf_op jit(solution)/shard_map/ppermute | solution.py:499
  810.4 35.7 %collective-permute-start.20 = (bf16[352,1024]{1,0:T(8,128)(2,1)S(1)}, bf16[352,1024]{1,0:T(8,128)(2,1)}, u32[]{:S(2)}, u32[]{:S(2)}) collective-permute-start(bf16[352,1024]{1,0:T(8,128)(2,1)S(1)} %mix.47.piece_ref), channel_id=1, source_target_pairs={{0,4},{2,6},{4,0},{6,2},{1,5},{3,7},{5,1},{7,3}} | collective-permute-start | bytes 2162696 | tf_op jit(solution)/shard_map/ppermute | solution.py:499
  822.6 30.9 %collective-permute-start.28 = (bf16[352,1024]{1,0:T(8,128)(2,1)S(1)}, bf16[352,1024]{1,0:T(8,128)(2,1)S(1)}, u32[]{:S(2)}, u32[]{:S(2)}) collective-permute-start(bf16[352,1024]{1,0:T(8,128)(2,1)S(1)} %mix.47.piece_ref), channel_id=1, source_target_pairs={{0,2},{2,0},{4,6},{6,4},{1,3},{3,1},{5,7},{7,5}} | collective-permute-start | bytes 2162696 | tf_op jit(solution)/shard_map/ppermute | solution.py:498
  824.6 36.9 %collective-permute-start.18 = (bf16[352,1024]{1,0:T(8,128)(2,1)S(1)}, bf16[352,1024]{1,0:T(8,128)(2,1)}, u32[]{:S(2)}, u32[]{:S(2)}) collective-permute-start(bf16[352,1024]{1,0:T(8,128)(2,1)S(1)} %mix.49.piece_ref), channel_id=1, source_target_pairs={{0,4},{2,6},{4,0},{6,2},{1,5},{3,7},{5,1},{7,3}} | collective-permute-start | bytes 2162696 | tf_op jit(solution)/shard_map/ppermute | solution.py:499
  838.0 133.9 %collective-permute-start.39 = (bf16[1408,768]{1,0:T(8,128)(2,1)S(1)}, bf16[1408,768]{1,0:T(8,128)(2,1)}, u32[]{:S(2)}, u32[]{:S(2)}) collective-permute-start(bf16[1408,768]{1,0:T(8,128)(2,1)S(1)} %mix.42.piece_ref), channel_id=1, source_target_pairs={{0,2},{2,0},{4,6},{6,4},{1,3},{3,1},{5,7},{7,5}} | collective-permute-start | bytes 6488072 | tf_op jit(solution)/shard_map/ppermute | solution.py:498
  840.0 132.5 %collective-permute-start.45 = (bf16[1408,768]{1,0:T(8,128)(2,1)S(1)}, bf16[1408,768]{1,0:T(8,128)(2,1)S(1)}, u32[]{:S(2)}, u32[]{:S(2)}) collective-permute-start(bf16[1408,768]{1,0:T(8,128)(2,1)S(1)} %mix.42.piece_ref), channel_id=1, source_target_pairs={{0,4},{2,6},{4,0},{6,2},{1,5},{3,7},{5,1},{7,3}} | collective-permute-start | bytes 6488072 | tf_op jit(solution)/shard_map/ppermute | solution.py:499
  846.0 69.2 %collective-permute-start.27 = (bf16[352,1024]{1,0:T(8,128)(2,1)S(1)}, bf16[352,1024]{1,0:T(8,128)(2,1)S(1)}, u32[]{:S(2)}, u32[]{:S(2)}) collective-permute-start(bf16[352,1024]{1,0:T(8,128)(2,1)S(1)} %mix.49.piece_ref), channel_id=1, source_target_pairs={{0,2},{2,0},{4,6},{6,4},{1,3},{3,1},{5,7},{7,5}} | collective-permute-start | bytes 2162696 | tf_op jit(solution)/shard_map/ppermute | solution.py:498
  854.3 68.9 %collective-permute-start.16 = (bf16[352,1024]{1,0:T(8,128)(2,1)S(1)}, bf16[352,1024]{1,0:T(8,128)(2,1)}, u32[]{:S(2)}, u32[]{:S(2)}) collective-permute-start(bf16[352,1024]{1,0:T(8,128)(2,1)S(1)} %mix.51.piece_ref), channel_id=1, source_target_pairs={{0,4},{2,6},{4,0},{6,2},{1,5},{3,7},{5,1},{7,3}} | collective-permute-start | bytes 2162696 | tf_op jit(solution)/shard_map/ppermute | solution.py:499
  861.5 65.0 %collective-permute-start.26 = (bf16[352,1024]{1,0:T(8,128)(2,1)S(1)}, bf16[352,1024]{1,0:T(8,128)(2,1)S(1)}, u32[]{:S(2)}, u32[]{:S(2)}) collective-permute-start(bf16[352,1024]{1,0:T(8,128)(2,1)S(1)} %mix.51.piece_ref), channel_id=1, source_target_pairs={{0,2},{2,0},{4,6},{6,4},{1,3},{3,1},{5,7},{7,5}} | collective-permute-start | bytes 2162696 | tf_op jit(solution)/shard_map/ppermute | solution.py:498
  916.2 22.5 %collective-permute-start.36 = (bf16[1408,256]{1,0:T(8,128)(2,1)S(1)}, bf16[1408,256]{1,0:T(8,128)(2,1)S(1)}, u32[]{:S(2)}, u32[]{:S(2)}) collective-permute-start(bf16[1408,256]{1,0:T(8,128)(2,1)S(1)} %collective-permute-done.35.piece_ref), channel_id=1, source_target_pairs={{0,4},{2,6},{4,0},{6,2},{1,5},{3,7},{5,1},{7,3}} | collective-permute-start | bytes 2162696 | tf_op jit(solution)/shard_map/ppermute | solution.py:499
  923.3 30.8 %collective-permute-start.34 = (bf16[1408,256]{1,0:T(8,128)(2,1)S(1)}, bf16[1408,256]{1,0:T(8,128)(2,1)S(1)}, u32[]{:S(2)}, u32[]{:S(2)}) collective-permute-start(bf16[1408,256]{1,0:T(8,128)(2,1)S(1)} %collective-permute-done.33.piece_ref), channel_id=1, source_target_pairs={{0,4},{2,6},{4,0},{6,2},{1,5},{3,7},{5,1},{7,3}} | collective-permute-start | bytes 2162696 | tf_op jit(solution)/shard_map/ppermute | solution.py:499
  927.4 42.1 %collective-permute-start.32 = (bf16[1408,256]{1,0:T(8,128)(2,1)S(1)}, bf16[1408,256]{1,0:T(8,128)(2,1)S(1)}, u32[]{:S(2)}, u32[]{:S(2)}) collective-permute-start(bf16[1408,256]{1,0:T(8,128)(2,1)S(1)} %collective-permute-done.31.piece_ref), channel_id=1, source_target_pairs={{0,4},{2,6},{4,0},{6,2},{1,5},{3,7},{5,1},{7,3}} | collective-permute-start | bytes 2162696 | tf_op jit(solution)/shard_map/ppermute | solution.py:499
  939.5 50.0 %collective-permute-start.37 = (bf16[1408,768]{1,0:T(8,128)(2,1)S(1)}, bf16[1408,768]{1,0:T(8,128)(2,1)}, u32[]{:S(2)}, u32[]{:S(2)}) collective-permute-start(bf16[1408,768]{1,0:T(8,128)(2,1)S(1)} %mix.44.piece_ref), channel_id=1, source_target_pairs={{0,2},{2,0},{4,6},{6,4},{1,3},{3,1},{5,7},{7,5}} | collective-permute-start | bytes 6488072 | tf_op jit(solution)/shard_map/ppermute | solution.py:498
  955.0 60.9 %collective-permute-start.44 = (bf16[1408,768]{1,0:T(8,128)(2,1)S(1)}, bf16[1408,768]{1,0:T(8,128)(2,1)S(1)}, u32[]{:S(2)}, u32[]{:S(2)}) collective-permute-start(bf16[1408,768]{1,0:T(8,128)(2,1)S(1)} %mix.44.piece_ref), channel_id=1, source_target_pairs={{0,4},{2,6},{4,0},{6,2},{1,5},{3,7},{5,1},{7,3}} | collective-permute-start | bytes 6488072 | tf_op jit(solution)/shard_map/ppermute | solution.py:499
  970.4 91.8 %collective-permute-start.24 = (bf16[352,3072]{1,0:T(8,128)(2,1)S(1)}, bf16[352,3072]{1,0:T(8,128)(2,1)S(1)}, u32[]{:S(2)}, u32[]{:S(2)}) collective-permute-start(bf16[352,3072]{1,0:T(8,128)(2,1)S(1)} %mix.43.piece_ref), channel_id=1, source_target_pairs={{0,4},{2,6},{4,0},{6,2},{1,5},{3,7},{5,1},{7,3}} | collective-permute-start | bytes 6488072 | tf_op jit(solution)/shard_map/ppermute | solution.py:499
  971.9 93.5 %collective-permute-start.30 = (bf16[352,3072]{1,0:T(8,128)(2,1)S(1)}, bf16[352,3072]{1,0:T(8,128)(2,1)}, u32[]{:S(2)}, u32[]{:S(2)}) collective-permute-start(bf16[352,3072]{1,0:T(8,128)(2,1)S(1)} %mix.43.piece_ref), channel_id=1, source_target_pairs={{0,2},{2,0},{4,6},{6,4},{1,3},{3,1},{5,7},{7,5}} | collective-permute-start | bytes 6488072 | tf_op jit(solution)/shard_map/ppermute | solution.py:498
  973.9 134.8 %collective-permute-start.22 = (bf16[352,3072]{1,0:T(8,128)(2,1)}, bf16[352,3072]{1,0:T(8,128)(2,1)}, u32[]{:S(2)}, u32[]{:S(2)}) collective-permute-start(bf16[352,3072]{1,0:T(8,128)(2,1)} %mix.45.piece_ref), channel_id=1, source_target_pairs={{0,4},{2,6},{4,0},{6,2},{1,5},{3,7},{5,1},{7,3}} | collective-permute-start | bytes 6488072 | tf_op jit(solution)/shard_map/ppermute | solution.py:499
  989.5 121.3 %collective-permute-start.29 = (bf16[352,3072]{1,0:T(8,128)(2,1)}, bf16[352,3072]{1,0:T(8,128)(2,1)}, u32[]{:S(2)}, u32[]{:S(2)}) collective-permute-start(bf16[352,3072]{1,0:T(8,128)(2,1)} %mix.45.piece_ref), channel_id=1, source_target_pairs={{0,2},{2,0},{4,6},{6,4},{1,3},{3,1},{5,7},{7,5}} | collective-permute-start | bytes 6488072 | tf_op jit(solution)/shard_map/ppermute | solution.py:498
  1017.3 137.7 %collective-permute-start.40 = (bf16[1408,768]{1,0:T(8,128)(2,1)}, bf16[1408,768]{1,0:T(8,128)(2,1)}, u32[]{:S(2)}, u32[]{:S(2)}) collective-permute-start(bf16[1408,768]{1,0:T(8,128)(2,1)} %collective-permute-done.39.piece_ref), channel_id=1, source_target_pairs={{0,4},{2,6},{4,0},{6,2},{1,5},{3,7},{5,1},{7,3}} | collective-permute-start | bytes 6488072 | tf_op jit(solution)/shard_map/ppermute | solution.py:499
  1063.6 133.0 %collective-permute-start.38 = (bf16[1408,768]{1,0:T(8,128)(2,1)}, bf16[1408,768]{1,0:T(8,128)(2,1)}, u32[]{:S(2)}, u32[]{:S(2)}) collective-permute-start(bf16[1408,768]{1,0:T(8,128)(2,1)} %collective-permute-done.37.piece_ref), channel_id=1, source_target_pairs={{0,4},{2,6},{4,0},{6,2},{1,5},{3,7},{5,1},{7,3}} | collective-permute-start | bytes 6488072 | tf_op jit(solution)/shard_map/ppermute | solution.py:499
  1065.4 288.6 %collective-permute-start.25 = (bf16[352,3072]{1,0:T(8,128)(2,1)}, bf16[352,3072]{1,0:T(8,128)(2,1)}, u32[]{:S(2)}, u32[]{:S(2)}) collective-permute-start(bf16[352,3072]{1,0:T(8,128)(2,1)} %copy-done.17), channel_id=1, source_target_pairs={{0,2},{2,0},{4,6},{6,4},{1,3},{3,1},{5,7},{7,5}} | collective-permute-start | bytes 6488072 | tf_op jit(solution)/shard_map/ppermute | solution.py:498
  1108.7 250.5 %collective-permute-start.23 = (bf16[352,3072]{1,0:T(8,128)(2,1)}, bf16[352,3072]{1,0:T(8,128)(2,1)}, u32[]{:S(2)}, u32[]{:S(2)}) collective-permute-start(bf16[352,3072]{1,0:T(8,128)(2,1)} %collective-permute-done.22.piece_ref), channel_id=1, source_target_pairs={{0,2},{2,0},{4,6},{6,4},{1,3},{3,1},{5,7},{7,5}} | collective-permute-start | bytes 6488072 | tf_op jit(solution)/shard_map/ppermute | solution.py:498
  1110.8 253.6 %collective-permute-start.21 = (bf16[352,1024]{1,0:T(8,128)(2,1)}, bf16[352,1024]{1,0:T(8,128)(2,1)}, u32[]{:S(2)}, u32[]{:S(2)}) collective-permute-start(bf16[352,1024]{1,0:T(8,128)(2,1)} %collective-permute-done.20.piece_ref), channel_id=1, source_target_pairs={{0,2},{2,0},{4,6},{6,4},{1,3},{3,1},{5,7},{7,5}} | collective-permute-start | bytes 2162696 | tf_op jit(solution)/shard_map/ppermute | solution.py:498
  1155.0 212.5 %collective-permute-start.19 = (bf16[352,1024]{1,0:T(8,128)(2,1)}, bf16[352,1024]{1,0:T(8,128)(2,1)}, u32[]{:S(2)}, u32[]{:S(2)}) collective-permute-start(bf16[352,1024]{1,0:T(8,128)(2,1)} %collective-permute-done.18.piece_ref), channel_id=1, source_target_pairs={{0,2},{2,0},{4,6},{6,4},{1,3},{3,1},{5,7},{7,5}} | collective-permute-start | bytes 2162696 | tf_op jit(solution)/shard_map/ppermute | solution.py:498
  1196.6 174.1 %collective-permute-start.17 = (bf16[352,1024]{1,0:T(8,128)(2,1)}, bf16[352,1024]{1,0:T(8,128)(2,1)}, u32[]{:S(2)}, u32[]{:S(2)}) collective-permute-start(bf16[352,1024]{1,0:T(8,128)(2,1)} %collective-permute-done.16.piece_ref), channel_id=1, source_target_pairs={{0,2},{2,0},{4,6},{6,4},{1,3},{3,1},{5,7},{7,5}} | collective-permute-start | bytes 2162696 | tf_op jit(solution)/shard_map/ppermute | solution.py:498
  (63 other events, 397.7 us)
